TPU v7x, 32 devices: a whole 2x2x4 slice. The times are simulated.
32 devices in a mesh: face: 4 (over z), tile: 4 (over y, core), lev: 2 (over x).
Axes of the slice: x: 2, y: 2, z: 4, core: 2. Of those that a mesh axis runs over, the one named last changes fastest.
Arguments:
- airflow_components: float32 [2, 36, 32, 512], P(None, 'lev', 'face', 'tile'), may hold values from -4.5 to 4.5, as said below
- heat_state: float32 [36, 32, 512], P('lev', 'face', 'tile'), may hold values from 0.5 to 2
- layer_pressure_depth: float32 [36, 32, 512], P('lev', 'face', 'tile'), may hold values from 0.5 to 2
- constituent_masses: float32 [18, 36, 32, 512], P(None, 'lev', 'face', 'tile'), may hold values from 0.1 to 1
- ground_gravity_potential: float32 [32, 512], P('face', 'tile'), may hold values from -8 to 8
- inverse_mapping_entries: float32 [4, 32, 512], P(None, 'face', 'tile'), may hold values from -4 to 4
- mapping_determinant: float32 [32, 512], P('face', 'tile'), may hold values from 0.5 to 2
- interface_rightangle_rotations: int32 [4, 4, 2], replicated, may hold values from 0 to 3
- interface_flipped_markers: int32 [4, 4, 2], replicated, may hold values from 0 to 1
- corner_block_tally: int32 [4, 4], replicated, may hold values from 3 to 4
Outputs:
- airflow_next: float32 [2, 36, 32, 512], P(None, 'lev', 'face', 'tile')
- heat_state_next: float32 [36, 32, 512], P('lev', 'face', 'tile')
- pressure_depth_next: float32 [36, 32, 512], P('lev', 'face', 'tile')
- constituent_masses_next: float32 [18, 36, 32, 512], P(None, 'lev', 'face', 'tile')
- stepping_bounds: float32 [2], replicated
Inputs may be any that keep to these rules, and one draw needn't show every extreme that they name: `airflow_components`: component magnitudes grow across the grid by up to a factor of 9. `interface_rightangle_rotations`: entry [f, t, 0] concerns the boundary between blocks (f, t) and (f+1, t), entry [f, t, 1] the one between (f, t) and (f, t+1). `interface_flipped_markers`: indexed like interface_rightangle_rotations. `corner_block_tally`: entry [f, t] belongs to the corner shared by blocks (f, t), (f+1, t), (f, t+1), (f+1, t+1).
All inputs are finite; a program needn't handle non-finite values.
Results may differ from a plain program's by a relative error of at most 0.00012.
Values sent between devices are 32-bit elements; how exact they have to be, the bound alone decides.
A program may use at most 64 MiB of HBM per device.

v0:
```python
import math

import jax
import jax.numpy as jnp
import numpy as np
from jax import lax
from jax.sharding import PartitionSpec as P

time_step = 0.05
viscosity = 0.05
highest = lax.Precision.HIGHEST


def carried_in(part, axis, combine, identity):
    count = lax.axis_size(axis)
    place = lax.axis_index(axis)
    ahead = count - 1 - place
    gathered = lax.all_gather(part, axis)
    state = jnp.zeros_like(part) + jnp.asarray(identity, part.dtype)

    def one(turn, state):
        source = count - 1 - turn
        return combine(state, lax.dynamic_index_in_dim(gathered, source, 0, False))

    return lax.fori_loop(0, ahead, one, state)


def extended(cells, sides, width):
    for axis, dim in sides:
        count = lax.axis_size(axis)
        head = lax.slice_in_dim(cells, 0, width, axis=dim)
        tail = lax.slice_in_dim(cells, cells.shape[dim] - width, cells.shape[dim], axis=dim)
        cells = jnp.concatenate(
            [
                lax.ppermute(tail, axis, [(i, (i + 1) % count) for i in range(count)]),
                cells,
                lax.ppermute(head, axis, [((i + 1) % count, i) for i in range(count)]),
            ],
            axis=dim,
        )
    return cells


def gll_tables():
    offset = 1.0 / math.sqrt(5.0)
    gll_nodes = np.array([-1.0, -offset, offset, 1.0])
    weights = np.array([1.0 / 6.0, 5.0 / 6.0, 5.0 / 6.0, 1.0 / 6.0])
    barycentric = np.ones(4)
    for outer_index in range(4):
        for inner_index in range(4):
            if inner_index != outer_index:
                barycentric[outer_index] = barycentric[outer_index] / (
                    gll_nodes[outer_index] - gll_nodes[inner_index]
                )
    derivative = np.zeros((4, 4))
    for outer_index in range(4):
        for inner_index in range(4):
            if inner_index != outer_index:
                derivative[outer_index, inner_index] = (
                    barycentric[inner_index]
                    / barycentric[outer_index]
                    / (gll_nodes[outer_index] - gll_nodes[inner_index])
                )
        derivative[outer_index, outer_index] = -np.sum(derivative[outer_index])
    return (derivative, weights)


def advance(
    east_wind,
    north_wind,
    temp_field,
    thick_field,
    tracer_field,
    geo_field,
    inverse_mapping_entries,
    mapping_determinant,
    along_rows,
    along_columns,
):

    def gradient(scalar):
        first_part = along_rows(scalar)
        second_part = along_columns(scalar)
        return (
            inverse_mapping_entries[0] * first_part + inverse_mapping_entries[2] * second_part,
            inverse_mapping_entries[1] * first_part + inverse_mapping_entries[3] * second_part,
        )

    def divergence(east_part, north_part):
        first_flux = mapping_determinant * (
            inverse_mapping_entries[0] * east_part + inverse_mapping_entries[1] * north_part
        )
        second_flux = mapping_determinant * (
            inverse_mapping_entries[2] * east_part + inverse_mapping_entries[3] * north_part
        )
        return (along_rows(first_flux) + along_columns(second_flux)) / mapping_determinant

    energy = 0.5 * (east_wind * east_wind + north_wind * north_wind) + geo_field
    energy_x, energy_y = gradient(energy)
    temp_x, temp_y = gradient(temp_field)
    thick_x, thick_y = gradient(thick_field)
    laplace = divergence(thick_x, thick_y)
    new_east = east_wind - time_step * energy_x
    new_north = north_wind - time_step * energy_y
    new_temp = temp_field - time_step * (east_wind * temp_x + north_wind * temp_y)
    new_thick = (
        thick_field
        - time_step * divergence(thick_field * east_wind, thick_field * north_wind)
        + time_step * viscosity * laplace
    )
    new_tracer = tracer_field - time_step * divergence(
        tracer_field * east_wind, tracer_field * north_wind
    )
    spacing = jnp.sqrt(
        inverse_mapping_entries[0] * inverse_mapping_entries[0]
        + inverse_mapping_entries[1] * inverse_mapping_entries[1]
        + inverse_mapping_entries[2] * inverse_mapping_entries[2]
        + inverse_mapping_entries[3] * inverse_mapping_entries[3]
    )
    courant = jnp.max(
        time_step * jnp.sqrt(east_wind * east_wind + north_wind * north_wind) * spacing
    )
    damping = jnp.max(time_step * viscosity * jnp.abs(laplace))
    fields = jnp.concatenate(
        [new_east[None], new_north[None], new_temp[None], new_thick[None], new_tracer], 0
    )
    return (fields, courant, damping)


def turn(pieces, code):
    cosine = jnp.where(code == 0, 1.0, jnp.where(code == 2, -1.0, 0.0)).astype(jnp.float32)
    sine = jnp.where(code == 1, 1.0, jnp.where(code == 3, -1.0, 0.0)).astype(jnp.float32)
    first_part = cosine * pieces[0] - sine * pieces[1]
    second_part = sine * pieces[0] + cosine * pieces[1]
    return jnp.concatenate([first_part[None], second_part[None], pieces[2:]], 0)


def flip_edge(strip, flag):
    return jnp.where(flag[..., None] == 1, strip[..., ::-1], strip)


def fix_edge(strip, flag, code):
    return turn(flip_edge(strip, flag), code[..., None])


def assemble(
    inner, top_rim, bottom_rim, left_rim, right_rim, corner_ll, corner_lh, corner_hl, corner_hh
):
    first_row = jnp.concatenate([corner_ll[..., None], top_rim, corner_lh[..., None]], -1)
    last_row = jnp.concatenate([corner_hl[..., None], bottom_rim, corner_hh[..., None]], -1)
    middle = jnp.concatenate([left_rim[..., None], inner, right_rim[..., None]], -1)
    return jnp.concatenate([first_row[..., None, :], middle, last_row[..., None, :]], -2)


def shared_sums(padded):
    row_count = padded.shape[-2] - 2
    column_count = padded.shape[-1] - 2
    row_low = (jnp.arange(row_count) % 4 == 0)[:, None]
    row_high = (jnp.arange(row_count) % 4 == 3)[:, None]
    across = (
        padded[..., 1:-1, :]
        + jnp.where(row_low, padded[..., :-2, :], 0.0)
        + jnp.where(row_high, padded[..., 2:, :], 0.0)
    )
    column_low = jnp.arange(column_count) % 4 == 0
    column_high = jnp.arange(column_count) % 4 == 3
    return (
        across[..., 1:-1]
        + jnp.where(column_low, across[..., :-2], 0.0)
        + jnp.where(column_high, across[..., 2:], 0.0)
    )


def combine_block(pieces, mass_pieces, rotations, flips, valences):
    inner, top_rim, bottom_rim, left_rim, right_rim, corner_ll, corner_lh, corner_hl, corner_hh = (
        pieces
    )
    mass_inner, mass_top, mass_bottom, mass_left, mass_right, mass_ll, mass_lh, mass_hl, mass_hh = (
        mass_pieces
    )
    top_code, bottom_code, left_code, right_code = rotations
    top_flag, bottom_flag, left_flag, right_flag = flips
    valence_ll, valence_lh, valence_hl, valence_hh = valences
    fixed = assemble(
        inner,
        fix_edge(top_rim, top_flag, top_code),
        fix_edge(bottom_rim, bottom_flag, bottom_code),
        fix_edge(left_rim, left_flag, left_code),
        fix_edge(right_rim, right_flag, right_code),
        jnp.where(valence_ll == 4, turn(corner_ll, (top_code + left_code) % 4), 0.0),
        jnp.where(valence_lh == 4, turn(corner_lh, (top_code + right_code) % 4), 0.0),
        jnp.where(valence_hl == 4, turn(corner_hl, (bottom_code + left_code) % 4), 0.0),
        jnp.where(valence_hh == 4, turn(corner_hh, (bottom_code + right_code) % 4), 0.0),
    )
    mass_fixed = assemble(
        mass_inner,
        flip_edge(mass_top, top_flag),
        flip_edge(mass_bottom, bottom_flag),
        flip_edge(mass_left, left_flag),
        flip_edge(mass_right, right_flag),
        jnp.where(valence_ll == 4, mass_ll, 0.0),
        jnp.where(valence_lh == 4, mass_lh, 0.0),
        jnp.where(valence_hl == 4, mass_hl, 0.0),
        jnp.where(valence_hh == 4, mass_hh, 0.0),
    )
    return shared_sums(fixed) / shared_sums(mass_fixed)


def rim_pieces(padded):
    return (
        padded[:, :, 1:-1, 1:-1],
        padded[:, :, 0, 1:-1],
        padded[:, :, -1, 1:-1],
        padded[:, :, 1:-1, 0],
        padded[:, :, 1:-1, -1],
        padded[:, :, 0, 0],
        padded[:, :, 0, -1],
        padded[:, :, -1, 0],
        padded[:, :, -1, -1],
    )


def add_terms(earlier, later):
    return earlier + later


def on_device(
    airflow_components,
    heat_state,
    layer_pressure_depth,
    constituent_masses,
    ground_gravity_potential,
    inverse_mapping_entries,
    mapping_determinant,
    interface_rightangle_rotations,
    interface_flipped_markers,
    corner_block_tally,
):
    derivative, weights = gll_tables()
    row_count = mapping_determinant.shape[0]
    column_count = mapping_determinant.shape[1]
    row_table = jnp.asarray(np.kron(np.eye(row_count // 4), derivative), jnp.float32)
    column_table = jnp.asarray(np.kron(np.eye(column_count // 4), derivative).T, jnp.float32)

    def along_rows(field):
        return jnp.einsum("ab,...bc->...ac", row_table, field, precision=highest)

    def along_columns(field):
        return jnp.einsum("...ab,bc->...ac", field, column_table, precision=highest)

    strip_parts_sequence = heat_state * layer_pressure_depth
    local_total = jnp.sum(strip_parts_sequence, axis=0)
    higher = carried_in(local_total, "lev", add_terms, jnp.zeros_like(local_total))
    gravity_potential_altitude = (
        ground_gravity_potential
        + higher
        + (local_total - jnp.cumsum(strip_parts_sequence, axis=0))
        + 0.5 * strip_parts_sequence
    )
    fields, courant, damping = advance(
        airflow_components[0],
        airflow_components[1],
        heat_state,
        layer_pressure_depth,
        constituent_masses,
        gravity_potential_altitude,
        inverse_mapping_entries,
        mapping_determinant,
        along_rows,
        along_columns,
    )
    courant_all, damping_all = lax.pmax((courant, damping), ("face", "tile", "lev"))
    stepping_bounds = jnp.stack([courant_all, damping_all])
    weight_rows = jnp.asarray(np.tile(weights, row_count // 4), jnp.float32)
    weight_columns = jnp.asarray(np.tile(weights, column_count // 4), jnp.float32)
    mass = mapping_determinant * weight_rows[:, None] * weight_columns[None, :]
    weighted = fields * mass
    mass_block = mass[None, None]
    padded, padded_mass = (
        extended(weighted, (("face", 2), ("tile", 3)), 1),
        extended(mass_block, (("face", 2), ("tile", 3)), 1),
    )
    face_index = lax.axis_index("face")
    tile_index = lax.axis_index("tile")
    face_count = lax.axis_size("face")
    tile_count = lax.axis_size("tile")
    face_lower = (face_index + face_count - 1) % face_count
    tile_lower = (tile_index + tile_count - 1) % tile_count
    rotations = (
        (4 - interface_rightangle_rotations[face_lower, tile_index, 0]) % 4,
        interface_rightangle_rotations[face_index, tile_index, 0],
        (4 - interface_rightangle_rotations[face_index, tile_lower, 1]) % 4,
        interface_rightangle_rotations[face_index, tile_index, 1],
    )
    flips = (
        interface_flipped_markers[face_lower, tile_index, 0],
        interface_flipped_markers[face_index, tile_index, 0],
        interface_flipped_markers[face_index, tile_lower, 1],
        interface_flipped_markers[face_index, tile_index, 1],
    )
    valences = (
        corner_block_tally[face_lower, tile_lower],
        corner_block_tally[face_lower, tile_index],
        corner_block_tally[face_index, tile_lower],
        corner_block_tally[face_index, tile_index],
    )
    pieces = rim_pieces(padded)
    pieces = (weighted,) + pieces[1:]
    mass_pieces = rim_pieces(padded_mass)
    mass_pieces = (mass_block,) + mass_pieces[1:]
    substep_outcome = combine_block(pieces, mass_pieces, rotations, flips, valences)
    airflow_next = substep_outcome[0:2]
    heat_state_next = substep_outcome[2]
    pressure_depth_next = substep_outcome[3]
    constituent_masses_next = substep_outcome[4:]
    return (
        airflow_next,
        heat_state_next,
        pressure_depth_next,
        constituent_masses_next,
        stepping_bounds,
    )


def solution(mesh):
    in_specs = (
        P(None, "lev", "face", "tile"),
        P("lev", "face", "tile"),
        P("lev", "face", "tile"),
        P(None, "lev", "face", "tile"),
        P("face", "tile"),
        P(None, "face", "tile"),
        P("face", "tile"),
        P(),
        P(),
        P(),
    )
    out_specs = (
        P(None, "lev", "face", "tile"),
        P("lev", "face", "tile"),
        P("lev", "face", "tile"),
        P(None, "lev", "face", "tile"),
        P(),
    )
    return jax.shard_map(
        on_device, mesh=mesh, in_specs=in_specs, out_specs=out_specs, check_vma=False
    )
```

profile of v0, /device:TPU:1, one launch (start us, length us, event | category | flops | bytes accessed | tf_op | source)
XLA Modules:
  0.0 135.1 jit_solution(1238440231042481853)
XLA Ops:
  0.7 1.0 multiply_reduce_fusion.2
  1.7 1.1 convolution_bitcast_fusion.4
  2.9 1.1 convolution_bitcast_fusion.2
  4.0 3.9 %all-gather = f32[16,128]{1,0:T(8,128)S(1)} all-gather(f32[8,128]{1,0:T(8,128)S(1)} %multiply_reduce_fusion.2), channel_id=2, replica_groups=mesh['face'=4,'tile'=4,'lev'=2] {'lev'}, dimensions={0}, use_global_device_ids=true | all-gather | bytes 12288 | tf_op jit(solution)/shard_map/all_gather | solution.py:18
  8.0 1.1 fusion.98
  9.1 0.7 add.329
  9.8 1.2 fusion.32
  11.0 0.2 convolution_bitcast_fusion.5
  11.2 0.2 bitcast_dynamic-update-slice_fusion.2
  11.5 0.2 convolution_bitcast_fusion.3
  11.7 0.2 convolution_bitcast_fusion.1
  11.9 0.8 multiply_reduce_fusion
  12.8 0.2 bitcast_dynamic-update-slice_fusion
  13.1 0.2 fusion.29
  13.4 1.5 %convolution_bitcast_fusion = f32[18,18,8,128]{3,2,1,0:T(8,128)S(1)} fusion(f32[8,8,1,1]{1,0,3,2:T(8,128)S(1)} %copy-done.27, f32[18,18,8,128]{3,2,1,0:T(8,128)S(1)} %copy-done.25, f32[18,8,128]{2,1,0:T(8,128)S(1)} %get-tuple-element.84, f32[8,128]{1,0:T(8,128)S(1)} %get-tuple-element.105, f32[18,8,128]{2,1,0:T(8,128)S(1)} %get-tuple-element.82, ...), kind=kOutput, calls=%fused_computation.19 | convolution fusion | flops 33841152 | bytes 2814208 | tf_op jit(solution)/shard_map/ab,...bc->...ac/dot_general | solution.py:246
  14.9 1.4 %fusion.10 = f32[22,18,8,128]{3,2,1,0:T(8,128)S(1)} fusion(f32[22,18,8,128]{3,2,1,0:T(8,128)S(1)} %fusion.29, f32[18,18,8,128]{3,2,1,0:T(8,128)S(1)} %copy-done.25, f32[18,18,8,128]{3,2,1,0:T(8,128)S(1)} %convolution_bitcast_fusion, f32[128,128,1,1]{1,0,3,2:T(8,128)S(1)} %copy-done.26, f32[8,128]{1,0:T(8,128)S(1)} %get-tuple-element.104, ...), kind=kOutput, calls=%fused_computation.22 | convolution fusion | flops 512925696 | bytes 5537792 | tf_op jit(solution)/shard_map/...ab,bc->...ac/dot_general | solution.py:249
  16.4 0.2 fusion.92
  16.7 3.6 %collective-permute-start.1 = (f32[22,18,1,128]{3,2,1,0:T(1,128)S(1)}, f32[22,18,1,128]{3,2,1,0:T(1,128)S(1)}, u32[]{:S(2)}, u32[]{:S(2)}) collective-permute-start(f32[22,18,1,128]{3,2,1,0:T(1,128)S(1)} %get-tuple-element.77), channel_id=1, source_target_pairs={{8,0},{16,8},{24,16},{0,24},{9,1},{17,9},{25,17},{1,25},{10,2},{18... | collective-permute-start | bytes 608264 | tf_op jit(solution)/shard_map/ppermute | solution.py:37
  20.3 3.3 %collective-permute-start.5 = (f32[1,1,1,128]{3,2,1,0:T(1,128)S(1)}, f32[1,1,1,128]{3,2,1,0:T(1,128)S(1)}, u32[]{:S(2)}, u32[]{:S(2)}) collective-permute-start(f32[1,1,1,128]{3,2,1,0:T(1,128)S(1)} %get-tuple-element.115), channel_id=1, source_target_pairs={{8,0},{16,8},{24,16},{0,24},{9,1},{17,9},{25,17},{1,25},{10,2},{18... | collective-permute-start | bytes 1544 | tf_op jit(solution)/shard_map/ppermute | solution.py:37
  23.6 0.7 constant_dynamic-slice_fusion.6
  33.6 0.6 fusion.97
  39.4 0.6 multiply_reduce_fusion.1
  40.0 41.7 %all-reduce = (f32[1]{0:T(128)}, f32[1]{0:T(128)}) all-reduce(f32[1]{0:T(128)} %bitcast.84, f32[1]{0:T(128)} %bitcast.83), channel_id=1, replica_groups=mesh['face'=4,'tile'=4,'lev'=2] {'face','tile','lev'}, use_global_device_ids=true, to_apply=%region_7.8 | all-reduce | flops 2 | bytes 16 | tf_op jit(solution)/shard_map/pmax | solution.py:272
  81.7 1.8 %pad_maximum_fusion.14 = f32[2]{0:T(128)} fusion(f32[1]{0:T(128)} %get-tuple-element.70, f32[1]{0:T(128)} %get-tuple-element.71), kind=kLoop, calls=%fused_computation.193 | loop fusion | flops 2 | bytes 16 | tf_op jit(solution)/shard_map/stack | solution.py:273
  83.7 1.3 collective-permute-start.7
  85.0 2.1 %collective-permute-start.6 = (f32[1,1,10,1]{3,2,1,0:T(8,128)S(1)}, f32[1,1,10,1]{3,2,1,0:T(8,128)S(1)}, u32[]{:S(2)}, u32[]{:S(2)}) collective-permute-start(f32[1,1,10,1]{3,2,1,0:T(8,128)S(1)} %get-tuple-element.110), channel_id=1, source_target_pairs={{0,2},{2,4},{4,6},{6,0},{1,3},{3,5},{5,7},{7,1},{8,10},{10,12},{12... | collective-permute-start | bytes 128 | tf_op jit(solution)/shard_map/ppermute | solution.py:35
  87.2 1.3 collective-permute-done.7
  88.6 0.1 slice_reduce_fusion
  88.9 0.1 slice_reduce_fusion.1
  89.2 0.5 fusion.94
  90.4 0.6 fusion.93
  93.1 0.7 fusion.86
  93.7 0.6 pad_maximum_fusion.6
  94.4 3.9 %fusion.91 = (f32[22,18,10,1]{3,2,1,0:T(8,128)}, f32[22,18,10,1]{3,2,1,0:T(8,128)}) fusion(f32[22,18,10,128]{3,2,1,0:T(8,128)S(1)} %pad_maximum_fusion.6), kind=kLoop, calls=%fused_computation.199 | loop fusion | bytes 63360 | tf_op jit(solution)/shard_map/slice | solution.py:32
  98.3 3.3 %copy.225 = f32[22,18,10,1]{0,3,2,1:T(1,128)} copy(f32[22,18,10,1]{3,2,1,0:T(8,128)} %get-tuple-element.73) | data formatting | bytes 31680 | tf_op jit(solution)/shard_map/slice | solution.py:31
  101.9 3.3 %copy.220 = f32[22,18,10,1]{0,3,2,1:T(1,128)} copy(f32[22,18,10,1]{3,2,1,0:T(8,128)} %get-tuple-element.72) | data formatting | bytes 31680 | tf_op jit(solution)/shard_map/slice | solution.py:32
  105.2 1.7 %collective-permute-start.2 = (f32[22,18,10,1]{0,3,2,1:T(1,128)}, f32[22,18,10,1]{0,3,2,1:T(1,128)S(1)}, u32[]{:S(2)}, u32[]{:S(2)}) collective-permute-start(f32[22,18,10,1]{0,3,2,1:T(1,128)} %copy.220), channel_id=1, source_target_pairs={{0,2},{2,4},{4,6},{6,0},{1,3},{3,5},{5,7},{7,1},{8,10},{10,12},{12... | collective-permute-start | bytes 47528 | tf_op jit(solution)/shard_map/ppermute | solution.py:35
  107.0 0.6 multiply_subtract_fusion.1
  107.7 0.7 slice_bitcast_fusion.6
  108.4 0.7 subtract_bitcast_fusion.2
  109.2 0.2 copy.246
  109.5 0.7 slice_bitcast_fusion.7
  110.2 0.7 subtract_bitcast_fusion.3
  111.0 0.2 copy.245
  111.2 0.4 maximum_bitcast_fusion.1
  111.6 1.2 copy.247
  112.7 0.1 copy.227
  113.0 1.2 copy.231
  114.1 1.5 %slice.319 = f32[22,18,8,1]{0,3,2,1:T(1,128)} slice(f32[22,18,10,1]{0,3,2,1:T(1,128)} %copy-done.4), slice={[0:22], [0:18], [1:9], [0:1]} | slice | bytes 25344 | tf_op jit(solution)/shard_map/slice | solution.py:214
  115.7 1.0 copy.222
  116.7 0.7 rev.24
  117.4 0.9 broadcast_select_fusion.3
  118.3 2.3 %copy.230 = f32[22,18,8,1]{3,2,1,0:T(8,128)} copy(f32[22,18,8,1]{1,2,0,3:T(8,128)S(1)} %maximum_bitcast_fusion.2) | data formatting | bytes 25344 | tf_op jit(solution)/shard_map/broadcast_in_dim | solution.py:151
  120.6 0.8 broadcast_select_fusion.6
  121.5 0.9 copy.238
  122.4 0.8 broadcast_select_fusion.7
  123.2 0.9 copy.237
  124.2 1.5 %maximum_bitcast_fusion = f32[22,18,1,130]{3,0,2,1:T(8,128)S(1)} fusion(f32[22,18,1]{2,0,1:T(8,128)} %copy.238, f32[20,18,128]{2,0,1:T(8,128)S(1)} %slice.333, f32[1,18,128]{2,0,1:T(1,128)} %get-tuple-element.79, f32[1,18,128]{2,0,1:T(1,128)} %get-tuple-element.78, f32[22,18,1]{2,0,1:T(8,128)} %copy.237), kind=kLoop, calls=%fused_computation.64 | loop fusion | flops 205920 | bytes 411840 | tf_op jit(solution)/shard_map/broadcast_in_dim | solution.py:152
  125.7 0.4 copy.239
  126.2 5.5 %fusion.1 = f32[22,18,8,130]{3,2,1,0:T(8,128)S(1)} fusion(f32[22,18,1,130]{3,2,1,0:T(1,128)} %copy.247, f32[22,18,8,1]{3,2,1,0:T(8,128)S(1)} %copy.231, f32[22,18,8,128]{3,2,1,0:T(8,128)S(1)} %broadcast_multiply_fusion, f32[22,18,8,1]{3,2,1,0:T(8,128)S(1)} %copy-done, f32[22,18,1,130]{3,2,1,0:T(1,128)S(1)} %copy.239, pred[8]{0:T(512)(128)(4,1)S(1)} %copy-done.19, ...), kind=kLoop, calls=%fused_computation.3 | loop fusion | flops 4942080 | bytes 3706576 | tf_op jit(solution)/shard_map/add | solution.py:161
  131.7 0.9 fusion.5
  132.7 0.7 slice.360
  133.3 0.7 slice_bitcast_fusion
  134.0 1.1 slice.363
  (111 shorter events, 2.1 us)
Async XLA Ops:
  0.6 10.6 %copy-start.8 = (f32[128,128,1]{1,0,2:T(8,128)S(1)}, f32[128,128,1]{1,0,2:T(8,128)}, u32[]{:S(2)}) copy-start(f32[128,128,1]{1,0,2:T(8,128)} %constant.221) | copy-start | bytes 196612
  0.6 10.3 %copy-start.7 = (f32[8,8,1]{1,0,2:T(8,128)S(1)}, f32[8,8,1]{1,0,2:T(8,128)}, u32[]{:S(2)}) copy-start(f32[8,8,1]{1,0,2:T(8,128)} %constant.220) | copy-start | bytes 772
  0.7 10.8 %copy-start.2 = (f32[18,8,128]{2,1,0:T(8,128)S(1)}, f32[18,8,128]{2,1,0:T(8,128)}, u32[]{:S(2)}) copy-start(f32[18,8,128]{2,1,0:T(8,128)} %param.18) | copy-start | bytes 221188
  0.7 10.6 %copy-start.1 = (f32[2,18,8,128]{3,2,1,0:T(8,128)S(1)}, f32[2,18,8,128]{3,2,1,0:T(8,128)}, u32[]{:S(2)}) copy-start(f32[2,18,8,128]{3,2,1,0:T(8,128)} %param.16) | copy-start | bytes 442372
  0.7 10.5 %copy-start.11 = (f32[4,8,128]{2,1,0:T(8,128)S(1)}, f32[4,8,128]{2,1,0:T(8,128)}, u32[]{:S(2)}) copy-start(f32[4,8,128]{2,1,0:T(8,128)} %param.21) | copy-start | bytes 49156
  0.7 10.8 %copy-start.9 = (f32[8,128]{1,0:T(8,128)S(1)}, f32[8,128]{1,0:T(8,128)}, u32[]{:S(2)}) copy-start(f32[8,128]{1,0:T(8,128)} %param.22) | copy-start | bytes 12292
  4.0 8.8 %copy-start.3 = (f32[18,8,128]{2,1,0:T(8,128)S(1)}, f32[18,8,128]{2,1,0:T(8,128)}, u32[]{:S(2)}) copy-start(f32[18,8,128]{2,1,0:T(8,128)} %param.17) | copy-start | bytes 221188
  7.9 5.1 %copy-start.23 = (f32[128]{0:T(128)S(1)}, f32[128]{0:T(128)}, u32[]{:S(2)}) copy-start(f32[128]{0:T(128)} %constant.219.clone) | copy-start | bytes 1540
  8.0 5.1 %copy-start.24 = (f32[8]{0:T(128)S(1)}, f32[8]{0:T(128)}, u32[]{:S(2)}) copy-start(f32[8]{0:T(128)} %constant.218.clone) | copy-start | bytes 100
  9.8 3.6 %copy-start.25 = (f32[18,18,8,128]{3,2,1,0:T(8,128)S(1)}, f32[18,18,8,128]{3,2,1,0:T(8,128)}, u32[]{:S(2)}) copy-start(f32[18,18,8,128]{3,2,1,0:T(8,128)} %param.19) | copy-start | bytes 3981316
  9.8 3.6 %copy-start.27 = (f32[8,8,1,1]{1,0,3,2:T(8,128)S(1)}, f32[8,8,1,1]{1,0,3,2:T(8,128)}, u32[]{:S(2)}) copy-start(f32[8,8,1,1]{1,0,3,2:T(8,128)} %constant.222) | copy-start | bytes 772
  13.3 1.5 %copy-start.26 = (f32[128,128,1,1]{1,0,3,2:T(8,128)S(1)}, f32[128,128,1,1]{1,0,3,2:T(8,128)}, u32[]{:S(2)}) copy-start(f32[128,128,1,1]{1,0,3,2:T(8,128)} %constant.223) | copy-start | bytes 196612
  16.3 7.3 %copy-start.21 = (s32[4,4,2]{1,2,0:T(2,128)S(1)}, s32[4,4,2]{1,2,0:T(2,128)}, u32[]{:S(2)}) copy-start(s32[4,4,2]{1,2,0:T(2,128)} %param.24) | copy-start | bytes 388
  16.3 7.3 %copy-start.22 = (s32[4,4,2]{1,2,0:T(2,128)S(1)}, s32[4,4,2]{1,2,0:T(2,128)}, u32[]{:S(2)}) copy-start(s32[4,4,2]{1,2,0:T(2,128)} %param.23) | copy-start | bytes 388
  16.3 17.2 %copy-start.20 = (s32[4,4]{1,0:T(4,128)S(1)}, s32[4,4]{1,0:T(4,128)}, u32[]{:S(2)}) copy-start(s32[4,4]{1,0:T(4,128)} %param.25) | copy-start | bytes 196
  16.7 77.0 %collective-permute-start.1 = (f32[22,18,1,128]{3,2,1,0:T(1,128)S(1)}, f32[22,18,1,128]{3,2,1,0:T(1,128)S(1)}, u32[]{:S(2)}, u32[]{:S(2)}) collective-permute-start(f32[22,18,1,128]{3,2,1,0:T(1,128)S(1)} %get-tuple-element.77), channel_id=1, source_target_pairs={{8,0},{16,8},{24,16},{0,24},{9,1},{17,9},{25,17},{1,25},{10,2},{18... | collective-permute-start | bytes 608264 | tf_op jit(solution)/shard_map/ppermute | solution.py:37
  20.3 73.4 %collective-permute-start = (f32[22,18,1,128]{3,2,1,0:T(1,128)S(1)}, f32[22,18,1,128]{3,2,1,0:T(1,128)S(1)}, u32[]{:S(2)}, u32[]{:S(2)}) collective-permute-start(f32[22,18,1,128]{3,2,1,0:T(1,128)S(1)} %get-tuple-element.76), channel_id=1, source_target_pairs={{0,8},{8,16},{16,24},{24,0},{1,9},{9,17},{17,25},{25,1},{2,10},{10... | collective-permute-start | bytes 608264 | tf_op jit(solution)/shard_map/ppermute | solution.py:35
  20.3 63.2 %collective-permute-start.5 = (f32[1,1,1,128]{3,2,1,0:T(1,128)S(1)}, f32[1,1,1,128]{3,2,1,0:T(1,128)S(1)}, u32[]{:S(2)}, u32[]{:S(2)}) collective-permute-start(f32[1,1,1,128]{3,2,1,0:T(1,128)S(1)} %get-tuple-element.115), channel_id=1, source_target_pairs={{8,0},{16,8},{24,16},{0,24},{9,1},{17,9},{25,17},{1,25},{10,2},{18... | collective-permute-start | bytes 1544 | tf_op jit(solution)/shard_map/ppermute | solution.py:37
  23.6 60.0 %collective-permute-start.4 = (f32[1,1,1,128]{3,2,1,0:T(1,128)S(1)}, f32[1,1,1,128]{3,2,1,0:T(1,128)S(1)}, u32[]{:S(2)}, u32[]{:S(2)}) collective-permute-start(f32[1,1,1,128]{3,2,1,0:T(1,128)S(1)} %get-tuple-element.114), channel_id=1, source_target_pairs={{0,8},{8,16},{16,24},{24,0},{1,9},{9,17},{17,25},{25,1},{2,10},{10... | collective-permute-start | bytes 1544 | tf_op jit(solution)/shard_map/ppermute | solution.py:35
  33.5 60.8 %copy-start.16 = (pred[8]{0:T(512)(128)(4,1)}, pred[8]{0:T(512)(128)(4,1)S(1)}, u32[]{:S(2)}) copy-start(pred[8]{0:T(512)(128)(4,1)S(1)} %get-tuple-element.134) | copy-start | bytes 28
  33.5 60.8 %copy-start.18 = (pred[8]{0:T(512)(128)(4,1)}, pred[8]{0:T(512)(128)(4,1)S(1)}, u32[]{:S(2)}) copy-start(pred[8]{0:T(512)(128)(4,1)S(1)} %get-tuple-element.135) | copy-start | bytes 28
  33.6 60.8 %copy-start.12 = (pred[128]{0:T(512)(128)(4,1)}, pred[128]{0:T(512)(128)(4,1)S(1)}, u32[]{:S(2)}) copy-start(pred[128]{0:T(512)(128)(4,1)S(1)} %get-tuple-element.132) | copy-start | bytes 388
  33.6 60.8 %copy-start.14 = (pred[128]{0:T(512)(128)(4,1)}, pred[128]{0:T(512)(128)(4,1)S(1)}, u32[]{:S(2)}) copy-start(pred[128]{0:T(512)(128)(4,1)S(1)} %get-tuple-element.133) | copy-start | bytes 388
  83.7 4.9 %collective-permute-start.7 = (f32[1,1,10,1]{3,2,1,0:T(8,128)S(1)}, f32[1,1,10,1]{3,2,1,0:T(8,128)S(1)}, u32[]{:S(2)}, u32[]{:S(2)}) collective-permute-start(f32[1,1,10,1]{3,2,1,0:T(8,128)S(1)} %get-tuple-element.111), channel_id=1, source_target_pairs={{2,0},{4,2},{6,4},{0,6},{3,1},{5,3},{7,5},{1,7},{10,8},{12,10},{14... | collective-permute-start | bytes 128 | tf_op jit(solution)/shard_map/ppermute | solution.py:37
  85.0 3.9 %collective-permute-start.6 = (f32[1,1,10,1]{3,2,1,0:T(8,128)S(1)}, f32[1,1,10,1]{3,2,1,0:T(8,128)S(1)}, u32[]{:S(2)}, u32[]{:S(2)}) collective-permute-start(f32[1,1,10,1]{3,2,1,0:T(8,128)S(1)} %get-tuple-element.110), channel_id=1, source_target_pairs={{0,2},{2,4},{4,6},{6,0},{1,3},{3,5},{5,7},{7,1},{8,10},{10,12},{12... | collective-permute-start | bytes 128 | tf_op jit(solution)/shard_map/ppermute | solution.py:35
  101.6 6.1 %collective-permute-start.3 = (f32[22,18,10,1]{0,3,2,1:T(1,128)}, f32[22,18,10,1]{0,3,2,1:T(1,128)S(1)}, u32[]{:S(2)}, u32[]{:S(2)}) collective-permute-start(f32[22,18,10,1]{0,3,2,1:T(1,128)} %copy.225), channel_id=1, source_target_pairs={{2,0},{4,2},{6,4},{0,6},{3,1},{5,3},{7,5},{1,7},{10,8},{12,10},{14... | collective-permute-start | bytes 47528 | tf_op jit(solution)/shard_map/ppermute | solution.py:37
  105.2 4.3 %collective-permute-start.2 = (f32[22,18,10,1]{0,3,2,1:T(1,128)}, f32[22,18,10,1]{0,3,2,1:T(1,128)S(1)}, u32[]{:S(2)}, u32[]{:S(2)}) collective-permute-start(f32[22,18,10,1]{0,3,2,1:T(1,128)} %copy.220), channel_id=1, source_target_pairs={{0,2},{2,4},{4,6},{6,0},{1,3},{3,5},{5,7},{7,1},{8,10},{10,12},{12... | collective-permute-start | bytes 47528 | tf_op jit(solution)/shard_map/ppermute | solution.py:35
  107.7 1.4 %copy-start.5 = (f32[22,18,10,1]{0,3,2,1:T(1,128)}, f32[22,18,10,1]{0,3,2,1:T(1,128)S(1)}, u32[]{:S(2)}) copy-start(f32[22,18,10,1]{0,3,2,1:T(1,128)S(1)} %collective-permute-done.3) | copy-start | bytes 47524
  109.2 3.5 %copy-start.6 = (f32[22,18,10,1]{0,3,2,1:T(1,128)S(1)}, f32[22,18,10,1]{0,3,2,1:T(1,128)}, u32[]{:S(2)}) copy-start(f32[22,18,10,1]{0,3,2,1:T(1,128)} %copy-done.5) | copy-start | bytes 47524
  109.5 3.5 %copy-start.4 = (f32[22,18,10,1]{0,3,2,1:T(1,128)}, f32[22,18,10,1]{0,3,2,1:T(1,128)S(1)}, u32[]{:S(2)}) copy-start(f32[22,18,10,1]{0,3,2,1:T(1,128)S(1)} %collective-permute-done.2) | copy-start | bytes 47524
  120.6 5.5 %copy-start.17 = (pred[8]{0:T(512)(128)(4,1)S(1)}, pred[8]{0:T(512)(128)(4,1)}, u32[]{:S(2)}) copy-start(pred[8]{0:T(512)(128)(4,1)} %copy-done.16) | copy-start | bytes 28
  120.6 5.5 %copy-start.19 = (pred[8]{0:T(512)(128)(4,1)S(1)}, pred[8]{0:T(512)(128)(4,1)}, u32[]{:S(2)}) copy-start(pred[8]{0:T(512)(128)(4,1)} %copy-done.18) | copy-start | bytes 28
  124.1 2.0 %copy-start = (f32[22,18,8,1]{3,2,1,0:T(8,128)S(1)}, f32[22,18,8,1]{3,2,1,0:T(8,128)}, u32[]{:S(2)}) copy-start(f32[22,18,8,1]{3,2,1,0:T(8,128)} %copy.230) | copy-start | bytes 38020
  126.2 5.6 %copy-start.10 = (f32[8,128]{1,0:T(8,128)S(1)}, f32[8,128]{1,0:T(8,128)}, u32[]{:S(2)}) copy-start(f32[8,128]{1,0:T(8,128)} %fusion.86) | copy-start | bytes 12292
  126.2 5.6 %copy-start.13 = (pred[128]{0:T(512)(128)(4,1)S(1)}, pred[128]{0:T(512)(128)(4,1)}, u32[]{:S(2)}) copy-start(pred[128]{0:T(512)(128)(4,1)} %copy-done.12) | copy-start | bytes 388
  126.2 5.6 %copy-start.15 = (pred[128]{0:T(512)(128)(4,1)S(1)}, pred[128]{0:T(512)(128)(4,1)}, u32[]{:S(2)}) copy-start(pred[128]{0:T(512)(128)(4,1)} %copy-done.14) | copy-start | bytes 388
where the time goes:
time: 136 us; the launch traced here: 135 us
  blocking collectives  45.6 us (34%)
  local copies, waits for them, and re-layouts  29 us (21%)
  other arithmetic  20.4 us (15%)
  between operations  18.4 us (14%)
  starting transfers between devices  12 us (9%)
  matrix products  8.36 us (6%)
  waiting for transfers between devices  1.36 us (1%)
    pmax x1, blocking collectives, on_device(): lax.pmax((courant, damping), ('face', 'tile', 'lev'))  41.7 us
    ppermute x4, starting transfers between devices, extended(): lax.ppermute(head, axis, [((i + 1) % count, i) for i in range(count)])  8.26 us
    slice x5, local copies, waits for them, and re-layouts, extended(): lax.slice_in_dim(cells, cells.shape[dim] - width, cells.shape[dim], axis=...  7.51 us
    add x2, other arithmetic, shared_sums(): padded[..., 1:-1, :] + jnp.where(row_low, padded[..., :-2, :], 0.0)  5.6 us
    dot_general x6, matrix products, along_columns(): return jnp.einsum('...ab,bc->...ac', field, column_table, precision=highest)  4.93 us
    all_gather x1, blocking collectives, carried_in(): gathered = lax.all_gather(part, axis)  3.89 us
    ppermute x4, starting transfers between devices, extended(): lax.ppermute(tail, axis, [(i, (i + 1) % count) for i in range(count)])  3.77 us
    dot_general x6, matrix products, along_rows(): return jnp.einsum('ab,...bc->...ac', row_table, field, precision=highest)  3.43 us
  transfers between devices with their start and end apart: 8, of which 1 were waited for; matrix products, arithmetic and copies ran while one was open for 9% of the time, Pallas kernels for 0%

commit v1 on v0

v1 whole, which is shorter than its diff:
```python
import functools
import math

import jax
import jax.numpy as jnp
import numpy as np
from jax import lax
from jax.experimental import pallas as pl
from jax.experimental.pallas import tpu as pltpu
from jax.sharding import PartitionSpec as P

time_step = 0.05
viscosity = 0.05
f32 = jnp.float32
bf16 = jnp.bfloat16
MESH = pl.DeviceIdType.MESH
highest = lax.Precision.HIGHEST


def gll_tables():
    offset = 1.0 / math.sqrt(5.0)
    nodes = np.array([-1.0, -offset, offset, 1.0])
    weights = np.array([1.0 / 6.0, 5.0 / 6.0, 5.0 / 6.0, 1.0 / 6.0])
    bary = np.ones(4)
    for i in range(4):
        for j in range(4):
            if j != i:
                bary[i] = bary[i] / (nodes[i] - nodes[j])
    derivative = np.zeros((4, 4))
    for i in range(4):
        for j in range(4):
            if j != i:
                derivative[i, j] = bary[j] / bary[i] / (nodes[i] - nodes[j])
        derivative[i, i] = -np.sum(derivative[i])
    return derivative, weights


def lane_tables(columns):
    derivative, weights = gll_tables()
    d = np.kron(np.eye(columns // 4), derivative)
    s = np.eye(columns)
    for c in range(columns - 1):
        if c % 4 == 3:
            s[c, c + 1] = s[c + 1, c] = 1.0
    w = np.tile(weights, columns // 4)
    t = (-time_step * (d.T * w[None, :]) @ s).astype(np.float32)
    t_hi = jnp.asarray(t).astype(bf16)
    t_lo = (jnp.asarray(t) - t_hi.astype(f32)).astype(bf16)
    sb = jnp.asarray(s, bf16)
    return jnp.concatenate([sb, sb, t_hi, t_hi, t_lo], 0), jnp.asarray(d.T, f32), jnp.asarray(w[None, :], f32)


def split(x):
    hi = x.astype(bf16)
    return hi, (x - hi.astype(f32)).astype(bf16)


def layout(levels, tracers):
    group = 8 // math.gcd(levels, 8)
    chunks, q = [], 0
    while q < tracers:
        n = min(group, tracers - q)
        chunks.append((q * levels, -(-n * levels // 8) * 8, n * levels))
        q += n
    return chunks


def kernel(
    sizes, dims,
    wind_h, temp_h, thick_h, tracer_h, ground_h, maps_h, det_h, ops_h, dct_h, wc_h,
    rot_ref, flip_ref, tally_ref,
    wind_o, temp_o, thick_o, tracer_o, bound_o,
    wind, temp, thick, tracer, geo, ground, maps, det, ops, dct, wc,
    a_ref, b_ref, z_ref, pack, corner, total, peak,
    up_in, down_in, left_in, right_in, corner_in, total_in, peak_in,
    in_sem, up_s, up_r, down_s, down_r, left_s, left_r, right_s, right_r,
    corner_s, corner_r, total_s, total_r, peak_s, peak_r,
):
    nf, nt, nl = sizes
    levels, rows, columns, chunks, pad = dims
    derivative, weights = gll_tables()
    rep = [a - (a // 4) for a in range(rows)]
    distinct = rows - rows // 4 + 1
    face, tile, lev = lax.axis_index("face"), lax.axis_index("tile"), lax.axis_index("lev")
    f_up, f_dn = lax.rem(face + nf - 1, nf), lax.rem(face + 1, nf)
    t_lf, t_rt = lax.rem(tile + nt - 1, nt), lax.rem(tile + 1, nt)

    pieces = [(0, 2 * pad + 8, 1)]
    at = 2 * pad + 8
    for _, count, _ in chunks:
        pieces.append((at, count, 1))
        at += count
    pieces.append((at, 2 * pad, 2))
    first_pack = np.cumsum([0] + [p[2] for p in pieces]).tolist()
    last = len(pieces) - 1

    local = [
        (temp_h, temp.at[: levels * rows]), (thick_h, thick.at[: levels * rows]),
        (wind_h.at[0], wind.at[0, : levels * rows]), (wind_h.at[1], wind.at[1, : levels * rows]),
        (maps_h, maps), (det_h, det), (wc_h, wc), (ground_h, ground), (dct_h, dct), (ops_h, ops),
    ]
    loads = [pltpu.make_async_copy(s, d, in_sem.at[i]) for i, (s, d) in enumerate(local)]
    n0 = len(local)
    for k, (start, _, valid) in enumerate(chunks):
        span = pl.ds(start * rows, valid * rows)
        loads.append(pltpu.make_async_copy(tracer_h.at[span], tracer.at[span], in_sem.at[n0 + k]))
    for load in loads:
        load.start()

    peers = [(lax.rem(face + o, nf), tile, lev) for o in range(1, nf)]
    peers += [(face, lax.rem(tile + o, nt), lev) for o in range(1, nt)]
    peers += [(face, tile, lax.rem(lev + o, nl)) for o in range(1, nl)]
    diagonals = [(f_dn, t_rt, lev), (f_dn, t_lf, lev), (f_up, t_rt, lev), (f_up, t_lf, lev)]
    barrier = pltpu.get_barrier_semaphore()
    for peer in peers + diagonals:
        pl.semaphore_signal(barrier, inc=1, device_id=peer, device_id_type=MESH)

    extra = (pad - levels) * rows
    if extra:
        zero = jnp.zeros((extra, columns), f32)
        temp[levels * rows :, :] = zero
        thick[levels * rows :, :] = zero
        geo[levels * rows :, :] = zero
        wind[0, levels * rows :, :] = zero
        wind[1, levels * rows :, :] = zero
    end = chunks[-1][0] + chunks[-1][2]
    more = chunks[-1][1] - chunks[-1][2]
    if more:
        tracer[end * rows :, :] = jnp.zeros((more * rows, columns), f32)

    sent = []

    def send(src, dst, s, r, to):
        copy = pltpu.make_async_remote_copy(
            src_ref=src, dst_ref=dst, send_sem=s, recv_sem=r, device_id=to, device_id_type=MESH
        )
        copy.start()
        sent.append(copy)
        return copy

    loads[0].wait()
    loads[1].wait()
    acc = jnp.zeros((rows, columns), f32)
    for k in reversed(range(levels)):
        term = temp[k * rows : (k + 1) * rows, :] * thick[k * rows : (k + 1) * rows, :]
        geo[k * rows : (k + 1) * rows, :] = acc + 0.5 * term
        acc = acc + term
    total[...] = acc
    pl.semaphore_wait(barrier, len(peers) + len(diagonals))
    totals = [
        send(total, total_in.at[o - 1], total_s.at[o - 1], total_r.at[o - 1],
             (face, tile, lax.rem(lev + o, nl)))
        for o in range(1, nl)
    ]

    for load in loads[2:n0]:
        load.wait()
    w_col = wc[...]
    table = ops[...]
    narrow = ops[: 2 * columns, :]
    wr = [float(weights[a % 4]) for a in range(rows)]
    m = [[maps[e * rows + a : e * rows + a + 1, :] for a in range(rows)] for e in range(4)]
    jac = [det[a : a + 1, :] for a in range(rows)]
    mass = [jac[a] * (wr[a] * w_col) for a in range(rows)]
    step_d = [[float(time_step * wr[a] * derivative[a % 4, b]) for b in range(4)] for a in range(rows)]
    dd = [[float(derivative[i, j]) for j in range(4)] for i in range(4)]

    def level_rows(ref, a):
        return ref[pl.ds(a, pad, stride=rows), :]

    def along_rows(values, a, coef):
        base = a - a % 4
        out = coef[0] * values[base]
        for b in range(1, 4):
            out = out + coef[b] * values[base + b]
        return out

    def merged(values):
        out = [None] * distinct
        for a in range(rows):
            r = rep[a]
            out[r] = values[a] if out[r] is None else out[r] + values[a]
        return out

    def lanes_plain(x):
        hi, lo = split(x)
        return jnp.dot(jnp.concatenate([hi, lo], 1), narrow, preferred_element_type=f32)

    def lanes_both(p, g):
        ph, plo = split(p)
        gh, glo = split(g)
        return jnp.dot(
            jnp.concatenate([ph, plo, gh, glo, gh], 1), table, preferred_element_type=f32
        )

    def by_column(values):
        stacked = jnp.concatenate(values, 0)
        out = jnp.dot(stacked, dct[...], precision=highest, preferred_element_type=f32)
        n = values[0].shape[0]
        return [out[i * n : (i + 1) * n] for i in range(len(values))]

    lane = lax.broadcasted_iota(jnp.int32, (8, columns), 1)
    unit = 2 * distinct
    within = lax.rem(lane, unit)

    def put(piece, offset, r, z):
        z_ref[r, piece + offset : piece + offset + z.shape[0], :] = z

    def pack_of(start, groups):
        out = jnp.zeros((8, columns), f32)
        for i in range(groups):
            for r in range(distinct):
                spot = unit * i + 2 * r
                value = pltpu.roll(z_ref[r, start + 8 * i : start + 8 * i + 8, :], spot + 1, 1)
                out = jnp.where((lane == spot) | (lane == spot + 1), value, out)
        return out

    def ship(j):
        start, count, packs = pieces[j]
        span = pl.ds(start, count)
        send(z_ref.at[distinct - 1, span], up_in.at[span], up_s.at[j], up_r.at[j], (f_dn, tile, lev))
        send(z_ref.at[0, span], down_in.at[span], down_s.at[j], down_r.at[j], (f_up, tile, lev))
        each = count // packs
        made = []
        for p in range(packs):
            made.append(pack_of(start + p * each, each // 8))
            pack[first_pack[j] + p] = made[-1]
        span = pl.ds(first_pack[j], packs)
        send(pack.at[span], left_in.at[span], left_s.at[j], left_r.at[j], (face, t_rt, lev))
        send(pack.at[span], right_in.at[span], right_s.at[j], right_r.at[j], (face, t_lf, lev))
        return made

    source = [unit - 2, unit - 1, 0, 1]

    def ship_corners(which, made):
        for d in range(4):
            out = jnp.zeros((8, columns), f32)
            for p, value in enumerate(made):
                out = jnp.where(within == p, pltpu.roll(value, (p - source[d]) % columns, 1), out)
            corner[which, d] = out
            send(corner.at[which, d], corner_in.at[which, d], corner_s.at[which, d],
                 corner_r.at[which, d], diagonals[d])

    east = [level_rows(wind.at[0], a) for a in range(rows)]
    north = [level_rows(wind.at[1], a) for a in range(rows)]
    speed = None
    whole = max(c[1] for c in chunks)
    for a in range(rows):
        aa = jac[a] * (m[0][a] * east[a] + m[1][a] * north[a])
        bb = jac[a] * (m[2][a] * east[a] + m[3][a] * north[a])
        aw, bw = (aa * w_col)[:levels], (bb * wr[a])[:levels]
        for k in range(-(-whole // levels)):
            n = min(levels, whole - k * levels)
            a_ref[a, k * levels : k * levels + n, :] = aw[:n]
            b_ref[a, k * levels : k * levels + n, :] = bw[:n]
        spacing = jnp.sqrt(
            m[0][a] * m[0][a] + m[1][a] * m[1][a] + m[2][a] * m[2][a] + m[3][a] * m[3][a]
        )
        here = jnp.max(east[a] * east[a] + north[a] * north[a], axis=0, keepdims=True)
        here = jnp.sqrt(here) * spacing
        speed = here if speed is None else jnp.maximum(speed, here)

    depth = [level_rows(thick, a) for a in range(rows)]
    depth_c = by_column(depth)
    flux_a, flux_b = [], []
    for a in range(rows):
        dr, dc = along_rows(depth, a, dd[a % 4]), depth_c[a]
        gx, gy = m[0][a] * dr + m[2][a] * dc, m[1][a] * dr + m[3][a] * dc
        flux_a.append(jac[a] * (m[0][a] * gx + m[1][a] * gy))
        flux_b.append(jac[a] * (m[2][a] * gx + m[3][a] * gy))
    flux_c = by_column(flux_b)
    damp = None
    for a in range(rows):
        lap = jnp.abs(along_rows(flux_a, a, dd[a % 4]) + flux_c[a])
        here = jnp.max(lap, axis=0, keepdims=True) / jac[a]
        damp = here if damp is None else jnp.maximum(damp, here)
    peak[0] = jnp.concatenate(
        [time_step * speed, (time_step * viscosity) * damp, jnp.zeros((6, columns), f32)], 0
    )
    peak_face = [
        send(peak.at[0], peak_in.at[o - 1], peak_s.at[o - 1], peak_r.at[o - 1],
             (lax.rem(face + o, nf), tile, lev))
        for o in range(1, nf)
    ]
    warm = [level_rows(temp, a) for a in range(rows)]
    warm_c = by_column(warm)
    value = []
    for a in range(rows):
        dr, dc = along_rows(warm, a, dd[a % 4]), warm_c[a]
        gx, gy = m[0][a] * dr + m[2][a] * dc, m[1][a] * dr + m[3][a] * dc
        value.append(mass[a] * (warm[a] - time_step * (east[a] * gx + north[a] * gy)))
    for r, x in enumerate(merged(value)):
        put(pieces[0][0], 0, r, lanes_plain(x))
    for r, x in enumerate(merged(mass)):
        put(pieces[0][0], pad, r, lanes_plain(jnp.broadcast_to(x, (8, columns))))
    first, second, keep = [], [], []
    for a in range(rows):
        aa = jac[a] * (m[0][a] * east[a] + m[1][a] * north[a])
        bb = jac[a] * (m[2][a] * east[a] + m[3][a] * north[a])
        first.append(w_col * (depth[a] * aa - viscosity * flux_a[a]))
        second.append(wr[a] * (depth[a] * bb - viscosity * flux_b[a]))
    for a in range(rows):
        keep.append(mass[a] * depth[a] - along_rows(first, a, step_d[a]))
    for r, (x, y) in enumerate(zip(merged(keep), merged(second))):
        put(pieces[0][0], pad + 8, r, lanes_both(x, y))
    made = ship(0)

    for k, (start, count, _) in enumerate(chunks):
        loads[n0 + k].wait()
        q = [tracer[pl.ds(start * rows + a, count, stride=rows), :] for a in range(rows)]
        first = [q[a] * a_ref[a, :count, :] for a in range(rows)]
        keep = [mass[a] * q[a] - along_rows(first, a, step_d[a]) for a in range(rows)]
        second = [q[a] * b_ref[a, :count, :] for a in range(rows)]
        for r, (x, y) in enumerate(zip(merged(keep), merged(second))):
            put(pieces[k + 1][0], 0, r, lanes_both(x, y))
        made += ship(k + 1)
    ship_corners(0, made)

    best = peak[0]
    for o, copy in enumerate(peak_face):
        copy.wait_recv()
        best = jnp.maximum(best, peak_in[o])
    peak[1] = best
    base = nf - 1
    peak_tile = [
        send(peak.at[1], peak_in.at[base + o - 1], peak_s.at[base + o - 1], peak_r.at[base + o - 1],
             (face, lax.rem(tile + o, nt), lev))
        for o in range(1, nt)
    ]

    above = ground[...]
    for o, copy in enumerate(totals):
        copy.wait_recv()
        origin = lax.rem(lev + nl - (o + 1), nl)
        use = jnp.where(origin > lev, 1.0, 0.0).astype(f32)
        above = above + use * total_in[o]
    energy = []
    for a in range(rows):
        u, v = level_rows(wind.at[0], a), level_rows(wind.at[1], a)
        energy.append(0.5 * (u * u + v * v) + level_rows(geo, a) + above[a : a + 1, :])
    energy_c = by_column(energy)
    value_u, value_v = [], []
    for a in range(rows):
        u, v = level_rows(wind.at[0], a), level_rows(wind.at[1], a)
        dr, dc = along_rows(energy, a, dd[a % 4]), energy_c[a]
        value_u.append(mass[a] * (u - time_step * (m[0][a] * dr + m[2][a] * dc)))
        value_v.append(mass[a] * (v - time_step * (m[1][a] * dr + m[3][a] * dc)))
    for r, (x, y) in enumerate(zip(merged(value_u), merged(value_v))):
        put(pieces[last][0], 0, r, lanes_plain(x))
        put(pieces[last][0], pad, r, lanes_plain(y))
    ship_corners(1, ship(last))

    best = peak[1]
    for o, copy in enumerate(peak_tile):
        copy.wait_recv()
        best = jnp.maximum(best, peak_in[base + o])
    peak[2] = best
    base = nf + nt - 2
    peak_lev = [
        send(peak.at[2], peak_in.at[base + o - 1], peak_s.at[base + o - 1], peak_r.at[base + o - 1],
             (face, tile, lax.rem(lev + o, nl)))
        for o in range(1, nl)
    ]

    def seam(ref, f, t, k):
        return ref[(f * nt + t) * 2 + k]

    codes = [
        lax.rem(4 - seam(rot_ref, f_up, tile, 0), 4), seam(rot_ref, face, tile, 0),
        lax.rem(4 - seam(rot_ref, face, t_lf, 1), 4), seam(rot_ref, face, tile, 1),
    ]
    flips = [
        seam(flip_ref, f_up, tile, 0), seam(flip_ref, face, tile, 0),
        seam(flip_ref, face, t_lf, 1), seam(flip_ref, face, tile, 1),
    ]
    tallies = [
        tally_ref[f_up * nt + t_lf], tally_ref[f_up * nt + tile],
        tally_ref[face * nt + t_lf], tally_ref[face * nt + tile],
    ]

    def cosine(code):
        return jnp.where(code == 0, 1.0, jnp.where(code == 2, -1.0, 0.0)).astype(f32)

    def sine(code):
        return jnp.where(code == 1, 1.0, jnp.where(code == 3, -1.0, 0.0)).astype(f32)

    def filled(x):
        return jnp.full((8, columns), x)

    odd = lax.rem(lane, 2) == 1
    mirror = lane - within + (unit - 2) - 2 * (within // 2) + lax.rem(within, 2)
    mirror = jnp.clip(mirror, 0, columns - 1)
    side_flip = jnp.where(odd, filled(flips[2]), filled(flips[3])) == 1
    side_cos = jnp.where(odd, filled(cosine(codes[2])), filled(cosine(codes[3])))
    side_sin = jnp.where(odd, filled(sine(codes[2])), filled(sine(codes[3])))
    corner_code = [
        lax.rem(codes[0] + codes[2], 4), lax.rem(codes[0] + codes[3], 4),
        lax.rem(codes[1] + codes[2], 4), lax.rem(codes[1] + codes[3], 4),
    ]
    target = [1, 0, unit - 1, unit - 2]
    alive = [filled(tallies[d]) == 4 for d in range(4)]

    def sides(index):
        a, b = left_in[index], right_in[index]
        x = jnp.where(odd, pltpu.roll(a, 1, 1), pltpu.roll(b, columns - 1, 1))
        return jnp.where(side_flip, jnp.take_along_axis(x, mirror, axis=1), x)

    def corner_values(which, d, p):
        x = pltpu.roll(corner_in[which, d], (target[d] - p) % columns, 1)
        return jnp.where(alive[d] & (within == target[d]), x, 0.0)

    edge = (lane[:1] == 0) | (lane[:1] == columns - 1)

    def to_edges(x, i, r):
        y = pltpu.roll(x, (columns - (unit * i + 2 * r + 1)) % columns, 1)
        return jnp.where(edge, y, 0.0)

    rev = (columns - 1) - lax.broadcasted_iota(jnp.int32, (8, columns), 1)
    row_flip = [filled(flips[0]) == 1, filled(flips[1]) == 1]

    def row_rim(ref, which, start, groups):
        out = []
        for i in range(groups):
            x = ref[start + 8 * i : start + 8 * i + 8, :]
            out.append(jnp.where(row_flip[which], jnp.take_along_axis(x, rev, axis=1), x))
        return out

    def arrived(j, corners):
        start, count, packs = pieces[j]
        span, pspan = pl.ds(start, count), pl.ds(first_pack[j], packs)

        def wait(src, dst, s, r, to):
            pltpu.make_async_remote_copy(
                src_ref=src, dst_ref=dst, send_sem=s, recv_sem=r, device_id=to, device_id_type=MESH
            ).wait_recv()

        wait(z_ref.at[distinct - 1, span], up_in.at[span], up_s.at[j], up_r.at[j], (f_dn, tile, lev))
        wait(z_ref.at[0, span], down_in.at[span], down_s.at[j], down_r.at[j], (f_up, tile, lev))
        wait(pack.at[pspan], left_in.at[pspan], left_s.at[j], left_r.at[j], (face, t_rt, lev))
        wait(pack.at[pspan], right_in.at[pspan], right_s.at[j], right_r.at[j], (face, t_lf, lev))
        if corners is not None:
            for d in range(4):
                wait(corner.at[corners, d], corner_in.at[corners, d], corner_s.at[corners, d],
                     corner_r.at[corners, d], diagonals[d])

    def finished(start, i, r, side, i_side, top, bottom):
        x = z_ref[r, start + 8 * i : start + 8 * i + 8, :] + to_edges(side, i_side, r)
        if r == 0:
            x = x + top
        if r == distinct - 1:
            x = x + bottom
        return x

    def store(ref, begin, i, valid, r, x):
        n = min(8, valid - 8 * i)
        if n <= 0:
            return
        for a in range(rows):
            if rep[a] == r:
                ref[pl.ds((begin + 8 * i) * rows + a, n, stride=rows), :] = (x * inverse[a])[:n]

    arrived(0, 0)
    x = sides(first_pack[0])
    for d in range(4):
        x = x + corner_values(0, d, 0)
    groups = pad // 8
    top, bottom = row_rim(up_in, 0, 0, 2 * groups + 1), row_rim(down_in, 1, 0, 2 * groups + 1)
    inverse = [None] * rows
    for r in range(distinct):
        whole_mass = 1.0 / finished(0, groups, r, x, groups, top[groups], bottom[groups])
        for a in range(rows):
            if rep[a] == r:
                inverse[a] = whole_mass
    for i in range(groups):
        for r in range(distinct):
            store(temp_o, 0, i, levels, r, finished(0, i, r, x, i, top[i], bottom[i]))
            j = groups + 1 + i
            store(thick_o, 0, i, levels, r, finished(0, j, r, x, j, top[j], bottom[j]))

    for k, (start, count, valid) in enumerate(chunks):
        j = k + 1
        arrived(j, None)
        x = sides(first_pack[j])
        for d in range(4):
            x = x + corner_values(0, d, j)
        top = row_rim(up_in, 0, pieces[j][0], count // 8)
        bottom = row_rim(down_in, 1, pieces[j][0], count // 8)
        for i in range(count // 8):
            for r in range(distinct):
                store(tracer_o, start, i, valid, r,
                      finished(pieces[j][0], i, r, x, i, top[i], bottom[i]))

    arrived(last, 1)
    p = first_pack[last]
    xu, xv = sides(p), sides(p + 1)
    xu, xv = side_cos * xu - side_sin * xv, side_sin * xu + side_cos * xv
    for d in range(4):
        cu, cv = corner_values(1, d, 0), corner_values(1, d, 1)
        c, s = cosine(corner_code[d]), sine(corner_code[d])
        xu, xv = xu + (c * cu - s * cv), xv + (s * cu + c * cv)
    begin = pieces[last][0]
    rims = []
    for which, ref in ((0, up_in), (1, down_in)):
        both = row_rim(ref, which, begin, 2 * groups)
        c, s = cosine(codes[which]), sine(codes[which])
        ru = [c * both[i] - s * both[groups + i] for i in range(groups)]
        rv = [s * both[i] + c * both[groups + i] for i in range(groups)]
        rims.append((ru, rv))
    for i in range(groups):
        for r in range(distinct):
            store(wind_o.at[0], 0, i, levels, r,
                  finished(begin, i, r, xu, i, rims[0][0][i], rims[1][0][i]))
            store(wind_o.at[1], 0, i, levels, r,
                  finished(begin + pad, i, r, xv, i, rims[0][1][i], rims[1][1][i]))

    best = peak[2]
    for o, copy in enumerate(peak_lev):
        copy.wait_recv()
        best = jnp.maximum(best, peak_in[base + o])
    bound_o[...] = jnp.broadcast_to(jnp.max(best, axis=1, keepdims=True), (8, columns))
    for copy in sent:
        copy.wait_send()


def on_device(
    sizes, wind, temp, thick, tracers, ground, maps, det, rot, flip, tally
):
    nf, nt, nl = sizes
    levels, rows, columns = temp.shape
    if rows != 8 or columns != 128:
        raise ValueError("block shape")
    count = tracers.shape[0]
    chunks = layout(levels, count)
    pad = -(-levels // 8) * 8
    table, dct, w_col = lane_tables(columns)
    distinct = rows - rows // 4 + 1
    total_rows = 4 * pad + 8 + sum(c[1] for c in chunks)
    pieces = len(chunks) + 2
    packs = len(chunks) + 3
    whole = max(c[1] for c in chunks)
    n = levels * rows
    dma = pltpu.SemaphoreType.DMA
    peers = nf + nt + nl - 3
    hbm = pl.BlockSpec(memory_space=pl.ANY)
    smem = pl.BlockSpec(memory_space=pltpu.SMEM)
    vmem = pl.BlockSpec(memory_space=pltpu.VMEM)
    last = chunks[-1]
    outs = pl.pallas_call(
        functools.partial(kernel, sizes, (levels, rows, columns, chunks, pad)),
        out_shape=(
            jax.ShapeDtypeStruct((2, n, columns), f32),
            jax.ShapeDtypeStruct((n, columns), f32),
            jax.ShapeDtypeStruct((n, columns), f32),
            jax.ShapeDtypeStruct((count * n, columns), f32),
            jax.ShapeDtypeStruct((8, columns), f32),
        ),
        in_specs=[hbm] * 10 + [smem] * 3,
        out_specs=(vmem,) * 5,
        scratch_shapes=[
            pltpu.VMEM((2, pad * rows, columns), f32),
            pltpu.VMEM((pad * rows, columns), f32),
            pltpu.VMEM((pad * rows, columns), f32),
            pltpu.VMEM(((last[0] + last[1]) * rows, columns), f32),
            pltpu.VMEM((pad * rows, columns), f32),
            pltpu.VMEM((rows, columns), f32),
            pltpu.VMEM((4 * rows, columns), f32),
            pltpu.VMEM((rows, columns), f32),
            pltpu.VMEM(table.shape, bf16),
            pltpu.VMEM(dct.shape, f32),
            pltpu.VMEM((1, columns), f32),
            pltpu.VMEM((rows, whole, columns), f32),
            pltpu.VMEM((rows, whole, columns), f32),
            pltpu.VMEM((distinct, total_rows, columns), f32),
            pltpu.VMEM((packs, 8, columns), f32),
            pltpu.VMEM((2, 4, 8, columns), f32),
            pltpu.VMEM((rows, columns), f32),
            pltpu.VMEM((3, 8, columns), f32),
            pltpu.VMEM((total_rows, columns), f32),
            pltpu.VMEM((total_rows, columns), f32),
            pltpu.VMEM((packs, 8, columns), f32),
            pltpu.VMEM((packs, 8, columns), f32),
            pltpu.VMEM((2, 4, 8, columns), f32),
            pltpu.VMEM((nl - 1, rows, columns), f32),
            pltpu.VMEM((peers, 8, columns), f32),
            dma((10 + len(chunks),)),
        ]
        + [dma((pieces,))] * 8
        + [dma((2, 4))] * 2
        + [dma((nl - 1,))] * 2
        + [dma((peers,))] * 2,
        compiler_params=pltpu.CompilerParams(collective_id=0, has_side_effects=True),
    )(
        wind.reshape(2, n, columns), temp.reshape(n, columns), thick.reshape(n, columns),
        tracers.reshape(count * n, columns), ground, maps.reshape(4 * rows, columns), det,
        table, dct, w_col, rot.reshape(-1), flip.reshape(-1), tally.reshape(-1),
    )
    return (
        outs[0].reshape(wind.shape), outs[1].reshape(temp.shape), outs[2].reshape(thick.shape),
        outs[3].reshape(tracers.shape), outs[4][:2, 0],
    )


def solution(mesh):
    sizes = tuple(mesh.shape[name] for name in ("face", "tile", "lev"))
    level = P("lev", "face", "tile")
    stacked = P(None, "lev", "face", "tile")
    return jax.shard_map(
        functools.partial(on_device, sizes),
        mesh=mesh,
        in_specs=(stacked, level, level, stacked, P("face", "tile"), P(None, "face", "tile"),
                  P("face", "tile"), P(), P(), P()),
        out_specs=(stacked, level, level, stacked, P()),
        check_vma=False,
    )
```

time: 136 us -> 36.6 us (0.27)
  blocking collectives: 45.6 us -> 0 us
  Pallas kernels: 0 us -> 23.1 us
  other arithmetic: 20.4 us -> 0 us
  between operations: 18.4 us -> 0.64 us
  local copies, waits for them, and re-layouts: 29 us -> 12.5 us
  starting transfers between devices: 12 us -> 0 us
  matrix products: 8.36 us -> 0 us
  waiting for transfers between devices: 1.36 us -> 0 us
    pmax x1 -> x0, blocking collectives: 41.7 us -> none  [on_device(): lax.pmax((courant, damping), ('face', 'tile', 'lev'))]
    pallas_call x0 -> x1, Pallas kernels: none -> 23.1 us  [on_device(): pl.pallas_call(functools.partial(kernel, sizes, (levels, rows, columns, c...]
    slice x18 -> x1, local copies, waits for them, and re-layouts: 15.5 us -> 1.3 us  [on_device(): outs[4][:2, 0]]
    ppermute x8 -> x0, starting transfers between devices: 12 us -> none  [the longest x4 8.26 us: extended(): lax.ppermute(head, axis, [((i + 1) % count, i) for i in range(count)])]
    unnamed x56 -> x6, local copies, waits for them, and re-layouts: 0.14 us -> 8.67 us
    dot_general x12 -> x0, matrix products: 8.36 us -> none  [the longest x6 4.93 us: along_columns(): return jnp.einsum('...ab,bc->...ac', field, column_table, precision=highest)]
    add x4 -> x0, other arithmetic: 6.3 us -> none  [the longest x2 5.6 us: shared_sums(): padded[..., 1:-1, :] + jnp.where(row_low, padded[..., :-2, :], 0.0)]
    broadcast_in_dim x7 -> x0, local copies, waits for them, and re-layouts: 5.26 us -> none  [the longest x2 2.42 us: assemble(): left_rim[..., None]]
  transfers between devices with their start and end apart: 8 -> 0, of which waited for: 1 -> 0; matrix products, arithmetic and copies ran while one was open for 9% -> 0% of each run, Pallas kernels for 0% -> 0%
where the time goes in v1:
time: 36.6 us; the launch traced here: 36.2 us
  Pallas kernels  23.1 us (63%)
  local copies, waits for them, and re-layouts  12.5 us (34%)
  between operations  0.64 us (2%)
    pallas_call x1, Pallas kernels, on_device(): pl.pallas_call(functools.partial(kernel, sizes, (levels, rows, columns, c...  23.1 us
    unnamed x6, local copies, waits for them, and re-layouts  8.67 us
    slice x1, local copies, waits for them, and re-layouts, on_device(): outs[4][:2, 0]  1.3 us
    reshape x1, local copies, waits for them, and re-layouts, on_device(): tally.reshape(-1)  1.27 us

profile of v1, /device:TPU:1, one launch (start us, length us, event | category | flops | bytes accessed | tf_op | source)
XLA Modules:
  0.0 36.2 jit_solution(896168141671624871)
XLA Ops:
  0.6 1.3 %reshape.53.tally_ref = s32[16]{0:T(128)} reshape(s32[4,4]{1,0:T(4,128)} %param.23) | data formatting | bytes 128 | tf_op jit(solution)/shard_map/reshape | solution.py:595
  1.9 0.8 %copy.21 = s32[4,4,2]{2,1,0:T(4,128)S(1)} copy(s32[4,4,2]{1,2,0:T(2,128)} %param.21) | data formatting | bytes 256 | tf_op args[7]
  2.7 0.6 %reshape.51.rot_ref = s32[32]{0:T(128)} reshape(s32[4,4,2]{2,1,0:T(4,128)S(1)} %copy.21) | data formatting | bytes 256 | tf_op jit(solution)/shard_map/reshape | solution.py:595
  3.3 0.8 %copy.22 = s32[4,4,2]{2,1,0:T(4,128)S(1)} copy(s32[4,4,2]{1,2,0:T(2,128)} %param.22) | data formatting | bytes 256 | tf_op args[8]
  4.1 0.6 %reshape.52.flip_ref = s32[32]{0:T(128)} reshape(s32[4,4,2]{2,1,0:T(4,128)S(1)} %copy.22) | data formatting | bytes 256 | tf_op jit(solution)/shard_map/reshape | solution.py:595
  4.7 23.1 %shard_map.173 = (f32[2,144,128]{2,1,0:T(8,128)}, f32[144,128]{1,0:T(8,128)}, f32[144,128]{1,0:T(8,128)}, f32[2592,128]{1,0:T(8,128)}, f32[8,128]{1,0:T(8,128)}) custom-call(f32[2,144,128]{2,1,0:T(8,128)} %bitcast.11, f32[144,128]{1,0:T(8,128)} %bitcast.13, f32[144,128]{1,0:T(8,128)} %bitcast.14, f32[2592,128]{1,0:T(8,128)} %bitcast.9, f32[8,128]{1,0:T(8,128)} %ground_h.1, ...), custom_call_target="tpu_custom_call" | custom-call | tf_op jit(solution)/shard_map/pallas_call | solution.py:548
  27.8 1.3 %slice_reduce_fusion = f32[2]{0:T(128)} fusion(f32[8,128]{1,0:T(8,128)} %get-tuple-element.14), kind=kLoop, calls=%fused_computation | loop fusion | bytes 16 | tf_op jit(solution)/shard_map/slice | solution.py:599
  29.1 1.6 %copy.27 = f32[2,18,8,128]{3,2,1,0:T(8,128)} copy(f32[2,18,8,128]{3,2,1,0:T(8,128)} %bitcast.12) | data formatting | bytes 294912
  30.7 1.5 %copy.28 = f32[18,8,128]{2,1,0:T(8,128)} copy(f32[18,8,128]{2,1,0:T(8,128)} %bitcast.16) | data formatting | bytes 147456
  32.2 1.5 %copy.29 = f32[18,8,128]{2,1,0:T(8,128)} copy(f32[18,8,128]{2,1,0:T(8,128)} %bitcast.15) | data formatting | bytes 147456
  33.7 2.5 %copy.30 = f32[18,18,8,128]{3,2,1,0:T(8,128)} copy(f32[18,18,8,128]{3,2,1,0:T(8,128)} %bitcast.10) | data formatting | bytes 2654208

commit v2 on v1

--- a/solution.py
+++ b/solution.py
@@ -363,7 +363,7 @@
     ]
 
     def seam(ref, f, t, k):
-        return ref[(f * nt + t) * 2 + k]
+        return ref[f, k, t]
 
     codes = [
         lax.rem(4 - seam(rot_ref, f_up, tile, 0), 4), seam(rot_ref, face, tile, 0),
@@ -374,8 +374,8 @@
         seam(flip_ref, face, t_lf, 1), seam(flip_ref, face, tile, 1),
     ]
     tallies = [
-        tally_ref[f_up * nt + t_lf], tally_ref[f_up * nt + tile],
-        tally_ref[face * nt + t_lf], tally_ref[face * nt + tile],
+        tally_ref[f_up, t_lf], tally_ref[f_up, tile],
+        tally_ref[face, t_lf], tally_ref[face, tile],
     ]
 
     def cosine(code):
@@ -517,9 +517,20 @@
     for o, copy in enumerate(peak_lev):
         copy.wait_recv()
         best = jnp.maximum(best, peak_in[base + o])
-    bound_o[...] = jnp.broadcast_to(jnp.max(best, axis=1, keepdims=True), (8, columns))
+    bound_o[...] = best
     for copy in sent:
         copy.wait_send()
+
+
+def write_out(wind, temp, thick, tracer, bound, wind_o, temp_o, thick_o, tracer_o, bound_o, sem):
+    pairs = ((tracer, tracer_o), (wind, wind_o), (temp, temp_o), (thick, thick_o))
+    copies = [pltpu.make_async_copy(a, b, sem.at[i]) for i, (a, b) in enumerate(pairs)]
+    for copy in copies:
+        copy.start()
+    bound_o[0] = jnp.max(bound[0:1, :])
+    bound_o[1] = jnp.max(bound[1:2, :])
+    for copy in copies:
+        copy.wait()
 
 
 def on_device(
@@ -545,15 +556,10 @@
     smem = pl.BlockSpec(memory_space=pltpu.SMEM)
     vmem = pl.BlockSpec(memory_space=pltpu.VMEM)
     last = chunks[-1]
+    shapes = ((2, n, columns), (n, columns), (n, columns), (count * n, columns), (8, columns))
     outs = pl.pallas_call(
         functools.partial(kernel, sizes, (levels, rows, columns, chunks, pad)),
-        out_shape=(
-            jax.ShapeDtypeStruct((2, n, columns), f32),
-            jax.ShapeDtypeStruct((n, columns), f32),
-            jax.ShapeDtypeStruct((n, columns), f32),
-            jax.ShapeDtypeStruct((count * n, columns), f32),
-            jax.ShapeDtypeStruct((8, columns), f32),
-        ),
+        out_shape=tuple(pltpu.VMEM(shape, f32) for shape in shapes),
         in_specs=[hbm] * 10 + [smem] * 3,
         out_specs=(vmem,) * 5,
         scratch_shapes=[
@@ -592,11 +598,18 @@
     )(
         wind.reshape(2, n, columns), temp.reshape(n, columns), thick.reshape(n, columns),
         tracers.reshape(count * n, columns), ground, maps.reshape(4 * rows, columns), det,
-        table, dct, w_col, rot.reshape(-1), flip.reshape(-1), tally.reshape(-1),
+        table, dct, w_col, rot.transpose(0, 2, 1), flip.transpose(0, 2, 1), tally,
     )
+    outs = pl.pallas_call(
+        write_out,
+        out_shape=tuple(jax.ShapeDtypeStruct(x, f32) for x in shapes[:4] + ((2,),)),
+        in_specs=[vmem] * 5,
+        out_specs=(hbm,) * 4 + (smem,),
+        scratch_shapes=[dma((4,))],
+    )(*[pltpu.with_memory_space_constraint(x, pltpu.VMEM) for x in outs])
     return (
         outs[0].reshape(wind.shape), outs[1].reshape(temp.shape), outs[2].reshape(thick.shape),
-        outs[3].reshape(tracers.shape), outs[4][:2, 0],
+        outs[3].reshape(tracers.shape), outs[4],
     )
 
 

time: 36.6 us -> 24.5 us (0.67)
  local copies, waits for them, and re-layouts: 12.5 us -> 0 us
  Pallas kernels: 23.1 us -> 23.7 us
    unnamed x6 -> x0, local copies, waits for them, and re-layouts: 8.67 us -> none
    reshape x3 -> x0, local copies, waits for them, and re-layouts: 2.49 us -> none  [the longest x1 1.27 us: on_device(): tally.reshape(-1)]
    pallas_call x0 -> x1, Pallas kernels: none -> 1.7 us  [on_device(): pl.pallas_call(write_out, out_shape=tuple((jax.ShapeDtypeStruct(x, f32) f...]
    slice x1 -> x0, local copies, waits for them, and re-layouts: 1.3 us -> none  [on_device(): outs[4][:2, 0]]
    pallas_call x1, Pallas kernels: 23.1 us -> 22 us  [on_device(): pl.pallas_call(functools.partial(kernel, sizes, (levels, rows, columns, c...]
where the time goes in v2:
time: 24.5 us; the launch traced here: 24.4 us
  Pallas kernels  23.7 us (97%)
  between operations  0.64 us (3%)
    pallas_call x1, Pallas kernels, on_device(): pl.pallas_call(functools.partial(kernel, sizes, (levels, rows, columns, c...  22 us
    pallas_call x1, Pallas kernels, on_device(): pl.pallas_call(write_out, out_shape=tuple((jax.ShapeDtypeStruct(x, f32) f...  1.7 us

profile of v2, /device:TPU:1, one launch (start us, length us, event | category | flops | bytes accessed | tf_op | source)
XLA Modules:
  0.0 24.4 jit_solution(3174841927715177566)
XLA Ops:
  0.6 22.0 %shard_map.173 = (f32[2,144,128]{2,1,0:T(8,128)S(1)}, f32[144,128]{1,0:T(8,128)S(1)}, f32[144,128]{1,0:T(8,128)S(1)}, f32[2592,128]{1,0:T(8,128)S(1)}, f32[8,128]{1,0:T(8,128)S(1)}) custom-call(f32[2,144,128]{2,1,0:T(8,128)} %bitcast.12, f32[144,128]{1,0:T(8,128)} %bitcast.13, f32[144,128]{1,0:T(8,128)} %bitcast.14, f32[2592,128]{1,0:T(8,128)} %bitcast.11, ...), custom_call_target="tpu_custom_call" | custom-call | tf_op jit(solution)/shard_map/pallas_call | solution.py:560
  22.7 1.7 %shard_map.174 = (f32[2,144,128]{2,1,0:T(8,128)}, f32[144,128]{1,0:T(8,128)}, f32[144,128]{1,0:T(8,128)}, f32[2592,128]{1,0:T(8,128)}, f32[2]{0:T(128)}) custom-call(f32[2,144,128]{2,1,0:T(8,128)S(1)} %get-tuple-element.15.wind, f32[144,128]{1,0:T(8,128)S(1)} %get-tuple-element.16.temp, f32[144,128]{1,0:T(8,128)S(1)} %get-tuple-element.17.thick, ...), custom_call_target="tpu_custom_call" | custom-call | tf_op jit(solution)/shard_map/pallas_call | solution.py:603

commit v3 on v2

--- a/solution.py
+++ b/solution.py
@@ -47,7 +47,10 @@
     t_hi = jnp.asarray(t).astype(bf16)
     t_lo = (jnp.asarray(t) - t_hi.astype(f32)).astype(bf16)
     sb = jnp.asarray(s, bf16)
-    return jnp.concatenate([sb, sb, t_hi, t_hi, t_lo], 0), jnp.asarray(d.T, f32), jnp.asarray(w[None, :], f32)
+    d_t = jnp.asarray(d.T, f32)
+    d_hi = d_t.astype(bf16)
+    d_lo = (d_t - d_hi.astype(f32)).astype(bf16)
+    return jnp.concatenate([sb, sb, t_hi, t_hi, t_lo], 0), jnp.concatenate([d_hi, d_hi, d_lo], 0), jnp.asarray(w[None, :], f32)
 
 
 def split(x):
@@ -85,14 +88,16 @@
     f_up, f_dn = lax.rem(face + nf - 1, nf), lax.rem(face + 1, nf)
     t_lf, t_rt = lax.rem(tile + nt - 1, nt), lax.rem(tile + 1, nt)
 
-    pieces = [(0, 2 * pad + 8, 1)]
-    at = 2 * pad + 8
+    pieces = [(0, 8, 1)]
+    at = 8
     for _, count, _ in chunks:
         pieces.append((at, count, 1))
         at += count
-    pieces.append((at, 2 * pad, 2))
+    pieces.append((at, 2 * pad, 1))
+    pieces.append((at + 2 * pad, 2 * pad, 2))
     first_pack = np.cumsum([0] + [p[2] for p in pieces]).tolist()
     last = len(pieces) - 1
+    heat = last - 1
 
     local = [
         (temp_h, temp.at[: levels * rows]), (thick_h, thick.at[: levels * rows]),
@@ -152,7 +157,6 @@
              (face, tile, lax.rem(lev + o, nl)))
         for o in range(1, nl)
     ]
-
     for load in loads[2:n0]:
         load.wait()
     w_col = wc[...]
@@ -195,7 +199,10 @@
 
     def by_column(values):
         stacked = jnp.concatenate(values, 0)
-        out = jnp.dot(stacked, dct[...], precision=highest, preferred_element_type=f32)
+        hi, lo = split(stacked)
+        out = jnp.dot(
+            jnp.concatenate([hi, lo, hi], 1), dct[...], preferred_element_type=f32
+        )
         n = values[0].shape[0]
         return [out[i * n : (i + 1) * n] for i in range(len(values))]
 
@@ -215,11 +222,14 @@
                 out = jnp.where((lane == spot) | (lane == spot + 1), value, out)
         return out
 
-    def ship(j):
-        start, count, packs = pieces[j]
+    def ship_rows(j):
+        start, count, _ = pieces[j]
         span = pl.ds(start, count)
         send(z_ref.at[distinct - 1, span], up_in.at[span], up_s.at[j], up_r.at[j], (f_dn, tile, lev))
         send(z_ref.at[0, span], down_in.at[span], down_s.at[j], down_r.at[j], (f_up, tile, lev))
+
+    def ship_sides(j):
+        start, count, packs = pieces[j]
         each = count // packs
         made = []
         for p in range(packs):
@@ -243,22 +253,36 @@
 
     east = [level_rows(wind.at[0], a) for a in range(rows)]
     north = [level_rows(wind.at[1], a) for a in range(rows)]
-    speed = None
+    speed, parts = None, []
     whole = max(c[1] for c in chunks)
     for a in range(rows):
         aa = jac[a] * (m[0][a] * east[a] + m[1][a] * north[a])
         bb = jac[a] * (m[2][a] * east[a] + m[3][a] * north[a])
-        aw, bw = (aa * w_col)[:levels], (bb * wr[a])[:levels]
-        for k in range(-(-whole // levels)):
-            n = min(levels, whole - k * levels)
-            a_ref[a, k * levels : k * levels + n, :] = aw[:n]
-            b_ref[a, k * levels : k * levels + n, :] = bw[:n]
+        parts.append(((aa * w_col)[:levels], (bb * wr[a])[:levels]))
         spacing = jnp.sqrt(
             m[0][a] * m[0][a] + m[1][a] * m[1][a] + m[2][a] * m[2][a] + m[3][a] * m[3][a]
         )
         here = jnp.max(east[a] * east[a] + north[a] * north[a], axis=0, keepdims=True)
         here = jnp.sqrt(here) * spacing
         speed = here if speed is None else jnp.maximum(speed, here)
+
+    @pl.when(face < nf)
+    def _():
+        for a, pair in enumerate(parts):
+            for k in range(-(-whole // levels)):
+                n = min(levels, whole - k * levels)
+                a_ref[a, k * levels : k * levels + n, :] = pair[0][:n]
+                b_ref[a, k * levels : k * levels + n, :] = pair[1][:n]
+
+    def tracers_of(k):
+        start, count, _ = chunks[k]
+        loads[n0 + k].wait()
+        q = [tracer[pl.ds(start * rows + a, count, stride=rows), :] for a in range(rows)]
+        first = [q[a] * a_ref[a, :count, :] for a in range(rows)]
+        keep = [mass[a] * q[a] - along_rows(first, a, step_d[a]) for a in range(rows)]
+        second = [q[a] * b_ref[a, :count, :] for a in range(rows)]
+        for r, (x, y) in enumerate(zip(merged(keep), merged(second))):
+            put(pieces[k + 1][0], 0, r, lanes_both(x, y))
 
     depth = [level_rows(thick, a) for a in range(rows)]
     depth_c = by_column(depth)
@@ -282,6 +306,30 @@
              (lax.rem(face + o, nf), tile, lev))
         for o in range(1, nf)
     ]
+
+    early = min(3, len(chunks))
+    for r, x in enumerate(merged(mass)):
+        put(0, 0, r, lanes_plain(jnp.broadcast_to(x, (8, columns))))
+    ship_rows(0)
+    ship_corners(0, ship_sides(0))
+    tracers_of(0)
+    ship_rows(1)
+    made = ship_sides(1)
+    for k in range(1, early):
+        tracers_of(k)
+        ship_rows(k + 1)
+        made += ship_sides(k + 1)
+
+    first, second, keep = [], [], []
+    for a in range(rows):
+        aa = jac[a] * (m[0][a] * east[a] + m[1][a] * north[a])
+        bb = jac[a] * (m[2][a] * east[a] + m[3][a] * north[a])
+        first.append(w_col * (depth[a] * aa - viscosity * flux_a[a]))
+        second.append(wr[a] * (depth[a] * bb - viscosity * flux_b[a]))
+    for a in range(rows):
+        keep.append(mass[a] * depth[a] - along_rows(first, a, step_d[a]))
+    for r, (x, y) in enumerate(zip(merged(keep), merged(second))):
+        put(pieces[heat][0], pad, r, lanes_both(x, y))
     warm = [level_rows(temp, a) for a in range(rows)]
     warm_c = by_column(warm)
     value = []
@@ -290,43 +338,13 @@
         gx, gy = m[0][a] * dr + m[2][a] * dc, m[1][a] * dr + m[3][a] * dc
         value.append(mass[a] * (warm[a] - time_step * (east[a] * gx + north[a] * gy)))
     for r, x in enumerate(merged(value)):
-        put(pieces[0][0], 0, r, lanes_plain(x))
-    for r, x in enumerate(merged(mass)):
-        put(pieces[0][0], pad, r, lanes_plain(jnp.broadcast_to(x, (8, columns))))
-    first, second, keep = [], [], []
-    for a in range(rows):
-        aa = jac[a] * (m[0][a] * east[a] + m[1][a] * north[a])
-        bb = jac[a] * (m[2][a] * east[a] + m[3][a] * north[a])
-        first.append(w_col * (depth[a] * aa - viscosity * flux_a[a]))
-        second.append(wr[a] * (depth[a] * bb - viscosity * flux_b[a]))
-    for a in range(rows):
-        keep.append(mass[a] * depth[a] - along_rows(first, a, step_d[a]))
-    for r, (x, y) in enumerate(zip(merged(keep), merged(second))):
-        put(pieces[0][0], pad + 8, r, lanes_both(x, y))
-    made = ship(0)
-
-    for k, (start, count, _) in enumerate(chunks):
-        loads[n0 + k].wait()
-        q = [tracer[pl.ds(start * rows + a, count, stride=rows), :] for a in range(rows)]
-        first = [q[a] * a_ref[a, :count, :] for a in range(rows)]
-        keep = [mass[a] * q[a] - along_rows(first, a, step_d[a]) for a in range(rows)]
-        second = [q[a] * b_ref[a, :count, :] for a in range(rows)]
-        for r, (x, y) in enumerate(zip(merged(keep), merged(second))):
-            put(pieces[k + 1][0], 0, r, lanes_both(x, y))
-        made += ship(k + 1)
-    ship_corners(0, made)
-
-    best = peak[0]
-    for o, copy in enumerate(peak_face):
-        copy.wait_recv()
-        best = jnp.maximum(best, peak_in[o])
-    peak[1] = best
-    base = nf - 1
-    peak_tile = [
-        send(peak.at[1], peak_in.at[base + o - 1], peak_s.at[base + o - 1], peak_r.at[base + o - 1],
-             (face, lax.rem(tile + o, nt), lev))
-        for o in range(1, nt)
-    ]
+        put(pieces[heat][0], 0, r, lanes_plain(x))
+    dynamic = ship_sides(heat)
+
+    for k in range(early, len(chunks)):
+        tracers_of(k)
+        made += ship_sides(k + 1)
+    ship_corners(1, made)
 
     above = ground[...]
     for o, copy in enumerate(totals):
@@ -348,19 +366,39 @@
     for r, (x, y) in enumerate(zip(merged(value_u), merged(value_v))):
         put(pieces[last][0], 0, r, lanes_plain(x))
         put(pieces[last][0], pad, r, lanes_plain(y))
-    ship_corners(1, ship(last))
-
-    best = peak[1]
-    for o, copy in enumerate(peak_tile):
-        copy.wait_recv()
-        best = jnp.maximum(best, peak_in[base + o])
-    peak[2] = best
-    base = nf + nt - 2
-    peak_lev = [
-        send(peak.at[2], peak_in.at[base + o - 1], peak_s.at[base + o - 1], peak_r.at[base + o - 1],
-             (face, tile, lax.rem(lev + o, nl)))
-        for o in range(1, nl)
-    ]
+    dynamic += ship_sides(last)
+    ship_corners(2, dynamic)
+    ship_rows(last)
+    for k in range(early, len(chunks)):
+        ship_rows(k + 1)
+    ship_rows(heat)
+
+    def second_stage():
+        best = peak[0]
+        for o, copy in enumerate(peak_face):
+            copy.wait_recv()
+            best = jnp.maximum(best, peak_in[o])
+        peak[1] = best
+        base = nf - 1
+        return [
+            send(peak.at[1], peak_in.at[base + o - 1], peak_s.at[base + o - 1],
+                 peak_r.at[base + o - 1], (face, lax.rem(tile + o, nt), lev))
+            for o in range(1, nt)
+        ]
+
+    def third_stage(peak_tile):
+        best = peak[1]
+        base = nf - 1
+        for o, copy in enumerate(peak_tile):
+            copy.wait_recv()
+            best = jnp.maximum(best, peak_in[base + o])
+        peak[2] = best
+        base = nf + nt - 2
+        return [
+            send(peak.at[2], peak_in.at[base + o - 1], peak_s.at[base + o - 1],
+                 peak_r.at[base + o - 1], (face, tile, lax.rem(lev + o, nl)))
+            for o in range(1, nl)
+        ]
 
     def seam(ref, f, t, k):
         return ref[f, k, t]
@@ -409,6 +447,7 @@
         x = pltpu.roll(corner_in[which, d], (target[d] - p) % columns, 1)
         return jnp.where(alive[d] & (within == target[d]), x, 0.0)
 
+    groups = pad // 8
     edge = (lane[:1] == 0) | (lane[:1] == columns - 1)
 
     def to_edges(x, i, r):
@@ -425,7 +464,7 @@
             out.append(jnp.where(row_flip[which], jnp.take_along_axis(x, rev, axis=1), x))
         return out
 
-    def arrived(j, corners):
+    def arrived(j, corners=None):
         start, count, packs = pieces[j]
         span, pspan = pl.ds(start, count), pl.ds(first_pack[j], packs)
 
@@ -460,29 +499,24 @@
                 ref[pl.ds((begin + 8 * i) * rows + a, n, stride=rows), :] = (x * inverse[a])[:n]
 
     arrived(0, 0)
-    x = sides(first_pack[0])
+    x = sides(0)
     for d in range(4):
         x = x + corner_values(0, d, 0)
-    groups = pad // 8
-    top, bottom = row_rim(up_in, 0, 0, 2 * groups + 1), row_rim(down_in, 1, 0, 2 * groups + 1)
+    top, bottom = row_rim(up_in, 0, 0, 1), row_rim(down_in, 1, 0, 1)
     inverse = [None] * rows
     for r in range(distinct):
-        whole_mass = 1.0 / finished(0, groups, r, x, groups, top[groups], bottom[groups])
+        whole_mass = 1.0 / finished(0, 0, r, x, 0, top[0], bottom[0])
         for a in range(rows):
             if rep[a] == r:
                 inverse[a] = whole_mass
-    for i in range(groups):
-        for r in range(distinct):
-            store(temp_o, 0, i, levels, r, finished(0, i, r, x, i, top[i], bottom[i]))
-            j = groups + 1 + i
-            store(thick_o, 0, i, levels, r, finished(0, j, r, x, j, top[j], bottom[j]))
-
-    for k, (start, count, valid) in enumerate(chunks):
+
+    def finish_tracers(k):
+        start, count, valid = chunks[k]
         j = k + 1
-        arrived(j, None)
+        arrived(j, 1 if k == 0 else None)
         x = sides(first_pack[j])
         for d in range(4):
-            x = x + corner_values(0, d, j)
+            x = x + corner_values(1, d, k)
         top = row_rim(up_in, 0, pieces[j][0], count // 8)
         bottom = row_rim(down_in, 1, pieces[j][0], count // 8)
         for i in range(count // 8):
@@ -490,12 +524,18 @@
                 store(tracer_o, start, i, valid, r,
                       finished(pieces[j][0], i, r, x, i, top[i], bottom[i]))
 
-    arrived(last, 1)
+    peak_tile = second_stage()
+    finish_tracers(0)
+    for k in range(1, early):
+        finish_tracers(k)
+    peak_lev = third_stage(peak_tile)
+
+    arrived(last, 2)
     p = first_pack[last]
     xu, xv = sides(p), sides(p + 1)
     xu, xv = side_cos * xu - side_sin * xv, side_sin * xu + side_cos * xv
     for d in range(4):
-        cu, cv = corner_values(1, d, 0), corner_values(1, d, 1)
+        cu, cv = corner_values(2, d, 1), corner_values(2, d, 2)
         c, s = cosine(corner_code[d]), sine(corner_code[d])
         xu, xv = xu + (c * cu - s * cv), xv + (s * cu + c * cv)
     begin = pieces[last][0]
@@ -513,6 +553,22 @@
             store(wind_o.at[1], 0, i, levels, r,
                   finished(begin + pad, i, r, xv, i, rims[0][1][i], rims[1][1][i]))
 
+    for k in range(early, len(chunks)):
+        finish_tracers(k)
+
+    arrived(heat)
+    begin = pieces[heat][0]
+    x = sides(first_pack[heat])
+    for d in range(4):
+        x = x + corner_values(2, d, 0)
+    top, bottom = row_rim(up_in, 0, begin, 2 * groups), row_rim(down_in, 1, begin, 2 * groups)
+    for i in range(groups):
+        for r in range(distinct):
+            store(temp_o, 0, i, levels, r, finished(begin, i, r, x, i, top[i], bottom[i]))
+            j = groups + i
+            store(thick_o, 0, i, levels, r, finished(begin, j, r, x, j, top[j], bottom[j]))
+
+    base = nf + nt - 2
     best = peak[2]
     for o, copy in enumerate(peak_lev):
         copy.wait_recv()
@@ -546,8 +602,8 @@
     table, dct, w_col = lane_tables(columns)
     distinct = rows - rows // 4 + 1
     total_rows = 4 * pad + 8 + sum(c[1] for c in chunks)
-    pieces = len(chunks) + 2
-    packs = len(chunks) + 3
+    pieces = len(chunks) + 3
+    packs = len(chunks) + 4
     whole = max(c[1] for c in chunks)
     n = levels * rows
     dma = pltpu.SemaphoreType.DMA
@@ -572,26 +628,26 @@
             pltpu.VMEM((4 * rows, columns), f32),
             pltpu.VMEM((rows, columns), f32),
             pltpu.VMEM(table.shape, bf16),
-            pltpu.VMEM(dct.shape, f32),
+            pltpu.VMEM(dct.shape, bf16),
             pltpu.VMEM((1, columns), f32),
             pltpu.VMEM((rows, whole, columns), f32),
             pltpu.VMEM((rows, whole, columns), f32),
             pltpu.VMEM((distinct, total_rows, columns), f32),
             pltpu.VMEM((packs, 8, columns), f32),
-            pltpu.VMEM((2, 4, 8, columns), f32),
+            pltpu.VMEM((3, 4, 8, columns), f32),
             pltpu.VMEM((rows, columns), f32),
             pltpu.VMEM((3, 8, columns), f32),
             pltpu.VMEM((total_rows, columns), f32),
             pltpu.VMEM((total_rows, columns), f32),
             pltpu.VMEM((packs, 8, columns), f32),
             pltpu.VMEM((packs, 8, columns), f32),
-            pltpu.VMEM((2, 4, 8, columns), f32),
+            pltpu.VMEM((3, 4, 8, columns), f32),
             pltpu.VMEM((nl - 1, rows, columns), f32),
             pltpu.VMEM((peers, 8, columns), f32),
             dma((10 + len(chunks),)),
         ]
         + [dma((pieces,))] * 8
-        + [dma((2, 4))] * 2
+        + [dma((3, 4))] * 2
         + [dma((nl - 1,))] * 2
         + [dma((peers,))] * 2,
         compiler_params=pltpu.CompilerParams(collective_id=0, has_side_effects=True),

time: 24.5 us -> 23.6 us (0.963)
  the two profiles are of different devices: /device:TPU:1 before, /device:TPU:0 now
where the time goes in v3:
time: 23.6 us; the launch traced here: 23.4 us
  Pallas kernels  22.8 us (97%)
  between operations  0.64 us (3%)
    pallas_call x1, Pallas kernels, on_device(): pl.pallas_call(functools.partial(kernel, sizes, (levels, rows, columns, c...  21.1 us
    pallas_call x1, Pallas kernels, on_device(): pl.pallas_call(write_out, out_shape=tuple((jax.ShapeDtypeStruct(x, f32) f...  1.7 us

profile of v3, /device:TPU:0, one launch (start us, length us, event | category | flops | bytes accessed | tf_op | source)
XLA Modules:
  0.0 23.4 jit_solution(2599626647929441817)
XLA Ops:
  0.6 21.1 %shard_map.173 = (f32[2,144,128]{2,1,0:T(8,128)S(1)}, f32[144,128]{1,0:T(8,128)S(1)}, f32[144,128]{1,0:T(8,128)S(1)}, f32[2592,128]{1,0:T(8,128)S(1)}, f32[8,128]{1,0:T(8,128)S(1)}) custom-call(f32[2,144,128]{2,1,0:T(8,128)} %bitcast.12, f32[144,128]{1,0:T(8,128)} %bitcast.13, f32[144,128]{1,0:T(8,128)} %bitcast.14, f32[2592,128]{1,0:T(8,128)} %bitcast.11, ...), custom_call_target="tpu_custom_call" | custom-call | tf_op jit(solution)/shard_map/pallas_call | solution.py:616
  21.8 1.7 %shard_map.174 = (f32[2,144,128]{2,1,0:T(8,128)}, f32[144,128]{1,0:T(8,128)}, f32[144,128]{1,0:T(8,128)}, f32[2592,128]{1,0:T(8,128)}, f32[2]{0:T(128)}) custom-call(f32[2,144,128]{2,1,0:T(8,128)S(1)} %get-tuple-element.15.wind, f32[144,128]{1,0:T(8,128)S(1)} %get-tuple-element.16.temp, f32[144,128]{1,0:T(8,128)S(1)} %get-tuple-element.17.thick, ...), custom_call_target="tpu_custom_call" | custom-call | tf_op jit(solution)/shard_map/pallas_call | solution.py:659
